TPU v7x, 256 devices: a whole 4x4x8 slice. The times are simulated.
256 devices in a mesh: rep: 64 (over y, z, core), shard: 4 (over x).
Axes of the slice: x: 4, y: 4, z: 8, core: 2. Of those that a mesh axis runs over, the one named last changes fastest.
Arguments:
- activ: bfloat16 [32768, 8192], P(('rep', 'shard')), may hold values from -6 to 6
- key_grad: bfloat16 [32768, 640], P(('rep', 'shard')), may hold values from -1.1953125 to 1.1953125
- key_weight: bfloat16 [8192, 640], P('shard'), may hold values from -0.25 to 0.25
- feedback: bfloat16 [64, 40960, 128], P('rep', 'shard'), may hold values from -24 to 24
- kept: int32 [64, 4, 512], P('rep', 'shard'), may hold values from 0 to 10239, as said below
- region_len: int32 [4, 64], P('shard'), may hold values from 80 to 240, as said below
Outputs:
- input_grad: bfloat16 [32768, 8192], P(('rep', 'shard'))
- next_feedback: bfloat16 [64, 40960, 128], P('rep', 'shard')
- owned_sum: float32 [4, 15360, 128], P('shard', 'rep')
Inputs may be any that keep to these rules, and one draw needn't show every extreme that they name: `region_len`: each row splits its shard's 10240 blocks into 64 regions in order of owner and sums to 10240; every row has a region of exactly 240 blocks. `kept`: the 512 numbers of a row are different blocks of that shard. At most 16 of them lie in one region of the shard; every row has exactly 16 in some region, and in every shard some region gets exactly 16 from every replica.
All inputs are finite; a program needn't handle non-finite values.
Results may differ from a plain program's by a relative error of at most 0.011.
Values may be sent and summed in bfloat16 or wider, within the bound.
No kernel may reach another device: no remote copies, remote signals or barrier semaphores. Data moves between devices by JAX's collectives and lax.ppermute only.
A program may use at most 128 MiB of HBM per device.

v0:
```python
import jax
import jax.numpy as jnp
from jax import lax
from jax.sharding import PartitionSpec as P


def in_order(tiles, dim):
    dims = list(tiles.shape[1:])
    dims[dim] *= tiles.shape[0]
    return jnp.moveaxis(tiles, 0, dim).reshape(dims)


def from_everyone(shard, axis):
    devices = lax.axis_size(axis)
    return lax.all_to_all(
        jnp.broadcast_to(shard[None], (devices, *shard.shape)), axis, 0, 0, tiled=True
    )


def gathered_copies(shard, axis, dim):
    return in_order(from_everyone(shard, axis), dim)


def accumulate(block_rows, block_ids, own_start, own_len, region_max):
    offset = block_ids - own_start
    inside = (offset >= 0) & (offset < own_len)
    target = jnp.where(inside, offset, region_max)
    blank = jnp.zeros((region_max, block_rows.shape[1]), jnp.float32)
    return blank.at[target].add(block_rows.astype(jnp.float32), mode="drop")


def per_device(activ, key_grad, key_weight, feedback, kept, region_len):
    grads_all = gathered_copies(key_grad, "shard", 0)
    act_cols = lax.all_to_all(activ, "shard", split_axis=1, concat_axis=0, tiled=True)
    weight_grad = lax.dot_general(
        act_cols, grads_all, (((0,), (0,)), ((), ())), preferred_element_type=jnp.float32
    )
    input_cols = lax.dot_general(
        grads_all, key_weight, (((1,), (1,)), ((), ())), preferred_element_type=jnp.float32
    ).astype(jnp.bfloat16)
    input_grad = lax.all_to_all(input_cols, "shard", split_axis=0, concat_axis=1, tiled=True)
    table = feedback[0]
    chosen = kept[0, 0]
    lengths = region_len[0]
    replicas = lax.axis_size("rep")
    block_count = table.shape[0]
    block_size = table.shape[1]
    keep_count = chosen.shape[0]
    mean_len = block_count // replicas
    region_max = mean_len + mean_len // 2
    starts = jnp.cumsum(lengths) - lengths
    owner_self = lax.axis_index("rep")
    own_start = starts[owner_self]
    own_len = lengths[owner_self]
    kept_rows = table[chosen]
    flags = jnp.zeros((block_count,), bool).at[chosen].set(True)
    cleared = jnp.where(flags[:, None], jnp.float32(0.0), table.astype(jnp.float32))
    next_feedback = (cleared + weight_grad.reshape(block_count, block_size)).astype(jnp.bfloat16)[
        None
    ]
    owner_id = jnp.sum((starts[None, :] <= chosen[:, None]).astype(jnp.int32), axis=1) - 1
    serial = jnp.arange(keep_count, dtype=jnp.int32)
    earlier = (owner_id[:, None] == owner_id[None, :]) & (serial[None, :] < serial[:, None])
    slot_index = jnp.sum(earlier.astype(jnp.int32), axis=1)
    capacity = 2 * keep_count // replicas
    place_at = owner_id * capacity + slot_index
    send_rows = (
        jnp.zeros((replicas * capacity, block_size), jnp.bfloat16).at[place_at].set(kept_rows)
    )
    send_ids = jnp.full((replicas * capacity,), -1, jnp.int32).at[place_at].set(chosen)
    got_rows, got_ids = (
        lax.all_to_all(send_rows, "rep", split_axis=0, concat_axis=0, tiled=True),
        lax.all_to_all(send_ids, "rep", split_axis=0, concat_axis=0, tiled=True),
    )
    owned_rows = accumulate(got_rows, got_ids, own_start, own_len, region_max)
    return (input_grad, next_feedback, owned_rows[None])


def solution(mesh):
    return jax.shard_map(
        per_device,
        mesh=mesh,
        in_specs=(
            P(("rep", "shard"), None),
            P(("rep", "shard"), None),
            P("shard", None),
            P("rep", "shard", None),
            P("rep", "shard", None),
            P("shard", None),
        ),
        out_specs=(P(("rep", "shard"), None), P("rep", "shard", None), P("shard", "rep", None)),
        check_vma=False,
    )
```

profile of v0, /device:TPU:8, one launch (start us, length us, event | category | flops | bytes accessed | tf_op | source)
XLA Modules:
  0.0 126.0 jit_solution(10083643363467482852)
XLA Ops:
  0.6 0.0 copy-start
  0.6 0.9 copy.21
  1.5 0.1 reduce-window.4
  1.6 0.1 reduce
  1.7 0.7 fusion.12
  2.4 0.8 convert_reduce_fusion.1
  3.2 0.2 convert_reduce_fusion
  3.5 2.6 %scatter_custom_fusion.1 = s32[1024]{0:T(1024)S(1)} fusion(s32[512]{0:T(512)S(1)} %bitcast.52, s32[512]{0:T(512)} %bitcast.50, s32[]{:T(128)} %constant.18.clone.1), kind=kCustom, calls=%fused_computation.28 | custom fusion | bytes 4608 | tf_op jit(solution)/shard_map/scatter | solution.py:70
  6.1 0.1 all_to_all.49
  6.2 20.6 %all_to_all.58 = s32[64,16,1]{1,2,0:T(1,128)} all-to-all(s32[64,16,1]{1,2,0:T(1,128)S(1)} %bitcast.44), channel_id=1, replica_groups=mesh['rep'=64,'shard'=4] {'rep'}, dimensions={0} | all-to-all | bytes 8192 | tf_op jit(solution)/shard_map/all_to_all | solution.py:73
  26.8 1.8 %broadcast_in_dim.30 = bf16[4,128,640]{2,1,0:T(8,128)(2,1)} broadcast(bf16[128,640]{1,0:T(8,128)(2,1)} %param.7), dimensions={1,2} | broadcast | bytes 819200 | tf_op jit(solution)/shard_map/broadcast_in_dim | solution.py:16
  28.6 4.3 %all-to-all-start = ((bf16[4,128,640]{2,1,0:T(8,128)(2,1)}), bf16[4,128,640]{2,1,0:T(8,128)(2,1)S(1)}, u32[]{:S(2)}, u32[]{:S(2)}) async-start(bf16[4,128,640]{2,1,0:T(8,128)(2,1)} %broadcast_in_dim.30), calls=%async_computation | async-start | bytes 1310720 | tf_op jit(solution)/shard_map/all_to_all | solution.py:15
  32.9 0.7 compare_select_fusion.2
  33.6 5.5 %scatter_custom_fusion.2 = bf16[1024,128]{1,0:T(8,128)(2,1)} fusion(s32[512]{0:T(512)S(1)} %bitcast.53, bf16[]{:T(256)} %constant.12.clone.1, bf16[10240,128]{1,0:T(8,128)(2,1)} %bitcast.39, s32[1024]{0:T(1024)S(1)} %pad_clamp_fusion), kind=kCustom, calls=%fused_computation.14 | custom fusion | bytes 262656 | tf_op jit(solution)/shard_map/scatter | solution.py:68
  39.1 4.6 %all-to-all-done = bf16[4,128,640]{2,1,0:T(8,128)(2,1)S(1)} async-done(((bf16[4,128,640]{2,1,0:T(8,128)(2,1)}), bf16[4,128,640]{2,1,0:T(8,128)(2,1)S(1)}, u32[]{:S(2)}, u32[]{:S(2)}) %all-to-all-start) | async-done | bytes 655392 | tf_op jit(solution)/shard_map/all_to_all | solution.py:15
  43.6 5.7 %all-to-all-start.4 = ((bf16[64,16,128]{2,1,0:T(8,128)(2,1)}), bf16[64,16,128]{2,1,0:T(8,128)(2,1)S(1)}, u32[]{:S(2)}, u32[]{:S(2)}) async-start(bf16[64,16,128]{2,1,0:T(8,128)(2,1)} %bitcast.19), calls=%async_computation.4 | async-start | bytes 524288 | tf_op jit(solution)/shard_map/all_to_all | solution.py:72
  49.3 4.1 %copy.20 = bf16[128,8192]{0,1:T(8,128)(2,1)} copy(bf16[128,8192]{1,0:T(8,128)(2,1)} %param.6) | data formatting | bytes 4194304 | tf_op args[0]
  53.4 0.0 copy-start.1
  53.4 7.5 %all-to-all-done.4 = bf16[64,16,128]{2,1,0:T(8,128)(2,1)S(1)} async-done(((bf16[64,16,128]{2,1,0:T(8,128)(2,1)}), bf16[64,16,128]{2,1,0:T(8,128)(2,1)S(1)}, u32[]{:S(2)}, u32[]{:S(2)}) %all-to-all-start.4) | async-done | bytes 262176 | tf_op jit(solution)/shard_map/all_to_all | solution.py:72
  60.8 4.5 %all-to-all-start.2 = ((bf16[128,4,2048]{0,2,1:T(8,128)(2,1)}), bf16[128,4,2048]{0,2,1:T(8,128)(2,1)}, u32[]{:S(2)}, u32[]{:S(2)}) async-start(bf16[128,4,2048]{0,2,1:T(8,128)(2,1)} %bitcast.38), calls=%async_computation.2 | async-start | bytes 4194304 | tf_op jit(solution)/shard_map/all_to_all | solution.py:34
  65.3 0.0 copy-done.1
  65.3 0.6 constant_dynamic-slice_fusion
  65.9 0.6 dynamic_slice.6
  66.5 0.5 broadcast.122
  67.0 2.8 %scatter_custom_fusion = pred[10240]{0:T(1024)(128)(4,1)S(1)} fusion(s32[512]{0:T(512)S(1)} %bitcast.47, pred[512]{0:T(512)(128)(4,1)} %broadcast.122, pred[]{:T(512)} %constant.13.clone.1), kind=kCustom, calls=%fused_computation.21 | custom fusion | bytes 10752 | tf_op jit(solution)/shard_map/scatter | solution.py:56
  69.8 2.1 %subtract_reduce_fusion = s32[64,16]{1,0:T(8,128)} fusion(s32[64,16,1]{1,2,0:T(1,128)} %all_to_all.58, s32[]{:T(128)} %bitcast.15), kind=kLoop, calls=%fused_computation.19 | loop fusion | flops 1024 | bytes 8196 | tf_op jit(solution)/shard_map/sub | solution.py:25
  71.9 0.8 sub.31
  72.7 1.2 compare_select_fusion
  73.9 0.0 copy-done
  73.9 3.1 %convolution_convert_fusion = bf16[512,2048]{1,0:T(8,128)(2,1)} fusion(bf16[512,640]{1,0:T(8,128)(2,1)S(1)} %bitcast.43, bf16[2048,640]{1,0:T(8,128)(2,1)S(1)} %copy-done), kind=kOutput, calls=%fused_computation.7 | convolution fusion | flops 1343225856 | bytes 5373952 | tf_op jit(solution)/shard_map/dot_general | solution.py:38
  77.1 6.8 %scatter_custom_fusion.3 = f32[240,128]{1,0:T(8,128)} fusion(s32[1024]{0:T(1024)} %bitcast.51, bf16[1024,128]{1,0:T(8,128)(2,1)S(1)} %bitcast.42, f32[]{:T(128)} %constant.17.clone.1), kind=kCustom, calls=%fused_computation.12 | custom fusion | flops 262144 | bytes 385536 | tf_op jit(solution)/shard_map/scatter-add | solution.py:29
  83.8 8.4 %all-to-all-done.2 = bf16[128,4,2048]{0,2,1:T(8,128)(2,1)} async-done(((bf16[128,4,2048]{0,2,1:T(8,128)(2,1)}), bf16[128,4,2048]{0,2,1:T(8,128)(2,1)}, u32[]{:S(2)}, u32[]{:S(2)}) %all-to-all-start.2) | async-done | bytes 2097184 | tf_op jit(solution)/shard_map/all_to_all | solution.py:34
  92.3 4.5 %all-to-all-start.1 = ((bf16[4,128,2048]{2,1,0:T(8,128)(2,1)}), bf16[4,128,2048]{2,1,0:T(8,128)(2,1)}, u32[]{:S(2)}, u32[]{:S(2)}) async-start(bf16[4,128,2048]{2,1,0:T(8,128)(2,1)} %bitcast.40), calls=%async_computation.1 | async-start | bytes 4194304 | tf_op jit(solution)/shard_map/all_to_all | solution.py:41
  96.8 5.7 %convolution_bitcast_fusion = f32[2048,640]{1,0:T(8,128)} fusion(bf16[4,128,640]{2,1,0:T(8,128)(2,1)S(1)} %all-to-all-done, bf16[128,4,2048]{0,2,1:T(8,128)(2,1)} %all-to-all-done.2), kind=kOutput, calls=%fused_computation.6 | convolution fusion | flops 1342177280 | bytes 7995392 | tf_op jit(solution)/shard_map/dot_general | solution.py:35
  102.5 6.5 %reshape.143 = f32[1,10240,128]{2,1,0:T(8,128)} reshape(f32[2048,640]{1,0:T(8,128)} %convolution_bitcast_fusion) | data formatting | bytes 10485760 | tf_op jit(solution)/shard_map/reshape | solution.py:58
  108.9 8.5 %add_convert_fusion = bf16[1,10240,128]{2,1,0:T(8,128)(2,1)} fusion(f32[1,10240,128]{2,1,0:T(8,128)} %reshape.143, bf16[1,10240,128]{2,1,0:T(8,128)(2,1)} %param.9, pred[10240]{0:T(1024)(128)(4,1)S(1)} %scatter_custom_fusion), kind=kLoop, calls=%fused_computation.5 | loop fusion | flops 5242880 | bytes 10496000 | tf_op jit(solution)/shard_map/convert_element_type | solution.py:58
  117.5 5.4 %all-to-all-done.1 = bf16[4,128,2048]{2,1,0:T(8,128)(2,1)} async-done(((bf16[4,128,2048]{2,1,0:T(8,128)(2,1)}), bf16[4,128,2048]{2,1,0:T(8,128)(2,1)}, u32[]{:S(2)}, u32[]{:S(2)}) %all-to-all-start.1) | async-done | bytes 2097184 | tf_op jit(solution)/shard_map/all_to_all | solution.py:41
  122.9 3.2 %copy.23 = bf16[4,16,8,2048]{3,2,0,1:T(8,128)(2,1)} copy(bf16[4,16,8,2048]{3,2,1,0:T(8,128)(2,1)} %bitcast.24) | data formatting | bytes 4194304 | tf_op jit(solution)/shard_map/all_to_all | solution.py:41
  (5 shorter events, 0.0 us)
Async XLA Ops:
  0.6 73.3 %copy-start = (bf16[2048,640]{1,0:T(8,128)(2,1)S(1)}, bf16[2048,640]{1,0:T(8,128)(2,1)}, u32[]{:S(2)}) copy-start(bf16[2048,640]{1,0:T(8,128)(2,1)} %param.8) | copy-start | bytes 7864324
  28.6 15.0 %all-to-all-start = ((bf16[4,128,640]{2,1,0:T(8,128)(2,1)}), bf16[4,128,640]{2,1,0:T(8,128)(2,1)S(1)}, u32[]{:S(2)}, u32[]{:S(2)}) async-start(bf16[4,128,640]{2,1,0:T(8,128)(2,1)} %broadcast_in_dim.30), calls=%async_computation | async-start | bytes 1310720 | tf_op jit(solution)/shard_map/all_to_all | solution.py:15
  43.6 17.2 %all-to-all-start.4 = ((bf16[64,16,128]{2,1,0:T(8,128)(2,1)}), bf16[64,16,128]{2,1,0:T(8,128)(2,1)S(1)}, u32[]{:S(2)}, u32[]{:S(2)}) async-start(bf16[64,16,128]{2,1,0:T(8,128)(2,1)} %bitcast.19), calls=%async_computation.4 | async-start | bytes 524288 | tf_op jit(solution)/shard_map/all_to_all | solution.py:72
  53.4 11.9 %copy-start.1 = (s32[1,64]{1,0:T(1,128)S(1)}, s32[1,64]{1,0:T(1,128)}, u32[]{:S(2)}) copy-start(s32[1,64]{1,0:T(1,128)} %param.11) | copy-start | bytes 772
  60.8 31.4 %all-to-all-start.2 = ((bf16[128,4,2048]{0,2,1:T(8,128)(2,1)}), bf16[128,4,2048]{0,2,1:T(8,128)(2,1)}, u32[]{:S(2)}, u32[]{:S(2)}) async-start(bf16[128,4,2048]{0,2,1:T(8,128)(2,1)} %bitcast.38), calls=%async_computation.2 | async-start | bytes 4194304 | tf_op jit(solution)/shard_map/all_to_all | solution.py:34
  92.3 30.6 %all-to-all-start.1 = ((bf16[4,128,2048]{2,1,0:T(8,128)(2,1)}), bf16[4,128,2048]{2,1,0:T(8,128)(2,1)}, u32[]{:S(2)}, u32[]{:S(2)}) async-start(bf16[4,128,2048]{2,1,0:T(8,128)(2,1)} %bitcast.40), calls=%async_computation.1 | async-start | bytes 4194304 | tf_op jit(solution)/shard_map/all_to_all | solution.py:41
where the time goes:
time: 127 us; the launch traced here: 126 us
  local copies, waits for them, and re-layouts  29.9 us (24%)
  waiting for transfers between devices  25.8 us (20%)
  other arithmetic  21.2 us (17%)
  blocking collectives  20.6 us (16%)
  starting transfers between devices  18.9 us (15%)
  matrix products  8.85 us (7%)
    all_to_all x1, blocking collectives, per_device(): lax.all_to_all(send_ids, 'rep', split_axis=0, concat_axis=0, tiled=True)  20.6 us
    convert_element_type x1, other arithmetic, per_device(): (cleared + weight_grad.reshape(block_count, block_size)).astype(jnp.bfloa...  8.55 us
    all_to_all x1, waiting for transfers between devices, per_device(): lax.all_to_all(activ, 'shard', split_axis=1, concat_axis=0, tiled=True)  8.43 us
    all_to_all x1, waiting for transfers between devices, per_device(): lax.all_to_all(send_rows, 'rep', split_axis=0, concat_axis=0, tiled=True)  7.46 us
    scatter-add x1, other arithmetic, accumulate(): return blank.at[target].add(block_rows.astype(jnp.float32), mode='drop')  6.79 us
    reshape x1, local copies, waits for them, and re-layouts, per_device(): weight_grad.reshape(block_count, block_size)  6.48 us
    dot_general x1, matrix products, per_device(): lax.dot_general(act_cols, grads_all, (((0,), (0,)), ((), ())), preferred_...  5.7 us
    all_to_all x1, starting transfers between devices, per_device(): lax.all_to_all(send_rows, 'rep', split_axis=0, concat_axis=0, tiled=True)  5.66 us
  transfers between devices with their start and end apart: 4, of which 4 were waited for; matrix products, arithmetic and copies ran while one was open for 39% of the time, Pallas kernels for 0%

commit v1 on v0

v1 whole, which is shorter than its diff:
```python
import jax
import jax.numpy as jnp
from jax import lax
from jax.experimental import pallas as pl
from jax.experimental.pallas import tpu as pltpu
from jax.sharding import PartitionSpec as P

BF = jnp.bfloat16
F32 = jnp.float32
VMEM = pltpu.VMEM
SMEM = pltpu.SMEM
SLOTS = 16
ROWS = 24
BUCKET = 64
GROUP = 8


def prep_kernel(me_ref, kept_ref, len_ref, table_ref, send_ref, clear_ref, wide, outbox, base, low, high, count):
    blocks = table_ref.shape[0]
    owners = send_ref.shape[0]
    chunk = 512

    def widen(i, carry):
        rows = pl.ds(pl.multiple_of(i * chunk, chunk), chunk)
        wide[rows, :] = table_ref[rows, :].astype(F32)
        return carry

    lax.fori_loop(0, blocks // chunk, widen, 0)
    outbox[...] = jnp.zeros_like(outbox)

    def reset(i, carry):
        count[i] = 0
        return carry

    lax.fori_loop(0, owners, reset, 0, unroll=8)

    def tabulate(b, carry):
        owner, first, last = carry
        step = last <= b * BUCKET
        owner = jnp.where(step, owner + 1, owner)
        first = jnp.where(step, last, first)
        last = jnp.where(step, last + len_ref[0, owner], last)
        base[b] = owner
        low[b] = first
        high[b] = last
        return owner, first, last

    lax.fori_loop(0, blocks // BUCKET, tabulate, (jnp.int32(0), jnp.int32(0), len_ref[0, 0]), unroll=4)

    lane = lax.broadcasted_iota(jnp.int32, (1, 128), 1)
    lane_base = lax.rem(me_ref[0], GROUP) * SLOTS
    blank = jnp.zeros((1, 128), F32)

    def move(k, carry):
        block = kept_ref[0, 0, k]
        bucket = lax.shift_right_logical(block, 6)
        split = high[bucket]
        after = block >= split
        owner = base[bucket] + after.astype(jnp.int32)
        offset = block - jnp.where(after, split, low[bucket])
        slot = count[owner]
        count[owner] = slot + 1
        row = owner * ROWS
        outbox[pl.ds(row + slot, 1), :] = wide[pl.ds(block, 1), :]
        wide[pl.ds(block, 1), :] = blank
        tag = pl.ds(row + SLOTS, 1)
        outbox[tag, :] = jnp.where(lane == lane_base + slot, (offset + 1).astype(F32), outbox[tag, :])
        return carry

    lax.fori_loop(0, kept_ref.shape[2], move, 0, unroll=8)

    def narrow(i, carry):
        rows = pl.ds(pl.multiple_of(i * chunk, chunk), chunk)
        clear_ref[rows, :] = wide[rows, :].astype(BF)
        return carry

    lax.fori_loop(0, blocks // chunk, narrow, 0)
    for o in range(owners):
        send_ref[o] = outbox[o * ROWS : (o + 1) * ROWS, :].astype(BF)


def prep(me, kept, lengths, table, owners):
    blocks, width = table.shape
    smem = pl.BlockSpec(memory_space=SMEM)
    vmem = pl.BlockSpec(memory_space=VMEM)
    return pl.pallas_call(
        prep_kernel,
        out_shape=(
            jax.ShapeDtypeStruct((owners, ROWS, width), BF),
            jax.ShapeDtypeStruct((blocks, width), BF),
        ),
        in_specs=[smem, smem, smem, vmem],
        out_specs=(vmem, vmem),
        scratch_shapes=[
            VMEM((blocks, width), F32),
            VMEM((owners * ROWS, width), F32),
            SMEM((blocks // BUCKET,), jnp.int32),
            SMEM((blocks // BUCKET,), jnp.int32),
            SMEM((blocks // BUCKET,), jnp.int32),
            SMEM((owners,), jnp.int32),
        ],
        compiler_params=pltpu.CompilerParams(vmem_limit_bytes=24 << 20),
        cost_estimate=pl.CostEstimate(flops=30_000_000, bytes_accessed=4 * blocks * width, transcendentals=0),
        name="prep",
    )(me, kept, lengths, table)


def owned_kernel(got_ref, out_ref):
    region_max = out_ref.shape[0]
    row_id = lax.broadcasted_iota(jnp.int32, (region_max, 128), 0).astype(F32) + 1.0
    total = jnp.zeros(out_ref.shape, F32)
    for g in range(got_ref.shape[0] // GROUP):
        part = got_ref[g * GROUP : (g + 1) * GROUP]
        tags = jnp.sum(part[:, SLOTS, :].astype(F32), axis=0, keepdims=True)
        pick = (row_id == tags).astype(F32).astype(BF)
        rows = part[:, :SLOTS, :].reshape(GROUP * SLOTS, 128)
        total += jnp.dot(pick, rows, preferred_element_type=F32)
    out_ref[...] = total


def owned(got, region_max):
    return pl.pallas_call(
        owned_kernel,
        out_shape=jax.ShapeDtypeStruct((region_max, got.shape[2]), F32),
        in_specs=[pl.BlockSpec(memory_space=VMEM)],
        out_specs=pl.BlockSpec(memory_space=VMEM),
        cost_estimate=pl.CostEstimate(flops=4_000_000, bytes_accessed=got.size * 2, transcendentals=0),
        name="owned",
    )(got)


def grad_kernel(my_ref, a0, a1, a2, a3, g0, g1, g2, g3, clear_ref, out_ref, spread):
    acts = jnp.concatenate([a0[...], a1[...], a2[...], a3[...]], axis=0)
    grads = jnp.concatenate([g0[...], g1[...], g2[...], g3[...]], axis=0)
    total = lax.dot_general(acts, grads, (((0,), (0,)), ((), ())), preferred_element_type=F32)
    tile, keys = total.shape
    per = keys // 128
    for j in range(per):
        spread[pl.ds(j, tile, stride=per), :] = total[:, j * 128 : (j + 1) * 128]
    out_ref[...] = (clear_ref[...].astype(F32) + spread[...]).astype(BF)


def grad_update(my, activ, pieces, grads, cleared):
    tile = 256
    tokens, features = pieces[0].shape
    keys = grads[0].shape[1]
    per = keys // 128
    steps = features // tile
    piece = pl.BlockSpec((tokens, tile), lambda t, my: (0, t))
    whole = pl.BlockSpec((tokens, keys), lambda t, my: (0, 0))
    rows = pl.BlockSpec((tile * per, 128), lambda t, my: (t, 0))
    return pl.pallas_call(
        grad_kernel,
        out_shape=jax.ShapeDtypeStruct(cleared.shape, BF),
        grid_spec=pltpu.PrefetchScalarGridSpec(
            num_scalar_prefetch=1,
            grid=(steps,),
            in_specs=[pl.BlockSpec((tokens, tile), lambda t, my: (0, my[0] * steps + t))]
            + [piece] * 3 + [whole] * 4 + [rows],
            out_specs=rows,
            scratch_shapes=[VMEM((tile * per, 128), F32)],
        ),
        compiler_params=pltpu.CompilerParams(vmem_limit_bytes=24 << 20),
        cost_estimate=pl.CostEstimate(
            flops=2 * 4 * tokens * features * keys, bytes_accessed=12 << 20, transcendentals=0
        ),
        name="grad_update",
    )(my, activ, *pieces, *grads, cleared)


def place_kernel(my_ref, p0, p1, p2, p3, out_ref, sems):
    width = p0.shape[1]
    copies = []
    for j, piece in enumerate((p0, p1, p2, p3)):
        column = lax.rem(my_ref[0] + 4 - j, 4) * width
        copy = pltpu.make_async_copy(
            piece, out_ref.at[:, pl.ds(pl.multiple_of(column, width), width)], sems.at[j]
        )
        copy.start()
        copies.append(copy)
    for copy in copies:
        copy.wait()


def place(my, pieces):
    tokens, width = pieces[0].shape
    return pl.pallas_call(
        place_kernel,
        out_shape=jax.ShapeDtypeStruct((tokens, 4 * width), BF),
        in_specs=[pl.BlockSpec(memory_space=SMEM)] + [pl.BlockSpec(memory_space=VMEM)] * 4,
        out_specs=pl.BlockSpec(memory_space=pl.ANY),
        scratch_shapes=[pltpu.SemaphoreType.DMA((4,))],
        compiler_params=pltpu.CompilerParams(vmem_limit_bytes=8 << 20),
        cost_estimate=pl.CostEstimate(flops=1_000_000, bytes_accessed=4 << 20, transcendentals=0),
        name="place",
    )(my, *pieces)


def shift(x, k, n=4):
    return lax.ppermute(x, "shard", [(i, (i + k) % n) for i in range(n)])


def nt_dot(a, b):
    return lax.dot_general(a, b, (((1,), (1,)), ((), ())), preferred_element_type=F32).astype(BF)


def per_device(activ, key_grad, key_weight, feedback, kept, region_len):
    shards = lax.axis_size("shard")
    my = lax.axis_index("shard")
    me = lax.axis_index("rep").reshape(1)
    my1 = my.reshape(1)
    owners = lax.axis_size("rep")
    width = activ.shape[1] // shards
    kgs = {k: shift(key_grad, k) for k in (1, 3, 2)}
    outgoing = {
        k: lax.dynamic_slice_in_dim(activ, lax.rem(my + k, shards) * width, width, axis=1) for k in (1, 3, 2)
    }
    acts = {k: shift(outgoing[k], k) for k in (1, 3, 2)}
    table = feedback[0]
    blocks = table.shape[0]
    mean_len = blocks // owners
    send, cleared = prep(me, kept, region_len, table, owners)
    got = lax.all_to_all(send, "rep", split_axis=0, concat_axis=0, tiled=True)
    own_part = nt_dot(key_grad, key_weight)
    back = {k: shift(nt_dot(kgs[k], key_weight), shards - k) for k in (1, 3, 2)}
    updated = grad_update(
        my1, activ, [acts[1], acts[2], acts[3]], [key_grad, kgs[1], kgs[2], kgs[3]], cleared
    )
    owned_rows = owned(got, mean_len + mean_len // 2)
    input_grad = place(my1, [own_part, back[3], back[2], back[1]])
    return (input_grad, updated[None], owned_rows[None])


def solution(mesh):
    return jax.shard_map(
        per_device,
        mesh=mesh,
        in_specs=(
            P(("rep", "shard"), None),
            P(("rep", "shard"), None),
            P("shard", None),
            P("rep", "shard", None),
            P("rep", "shard", None),
            P("shard", None),
        ),
        out_specs=(P(("rep", "shard"), None), P("rep", "shard", None), P("shard", "rep", None)),
        check_vma=False,
    )
```

time: 127 us -> 75.6 us (0.60)
  local copies, waits for them, and re-layouts: 29.9 us -> 6.55 us
  other arithmetic: 21.2 us -> 0 us
  blocking collectives: 20.6 us -> 0 us
  Pallas kernels: 0 us -> 17.4 us
  starting transfers between devices: 18.9 us -> 25.7 us
  waiting for transfers between devices: 25.8 us -> 20.5 us
  matrix products: 8.85 us -> 3.81 us
    all_to_all x4 -> x1, waiting for transfers between devices: 25.8 us -> 0.01 us  [per_device(): got = lax.all_to_all(send, 'rep', split_axis=0, concat_axis=0, tiled=True)]
    all_to_all x1 -> x0, blocking collectives: 20.6 us -> none  [per_device(): lax.all_to_all(send_ids, 'rep', split_axis=0, concat_axis=0, tiled=True)]
    ppermute x0 -> x9, waiting for transfers between devices: none -> 20.5 us  [shift(): return lax.ppermute(x, 'shard', [(i, (i + k) % n) for i in range(n)])]
    pallas_call x0 -> x4, Pallas kernels: none -> 17.4 us  [the longest x1 7.04 us: prep(): pl.pallas_call(prep_kernel, out_shape=(jax.ShapeDtypeStruct((owners, ROWS...]
    ppermute x0 -> x9, starting transfers between devices: none -> 13.6 us  [shift(): return lax.ppermute(x, 'shard', [(i, (i + k) % n) for i in range(n)])]
    scatter x3 -> x0, local copies, waits for them, and re-layouts: 10.9 us -> none  [the longest x1 5.5 us: per_device(): jnp.zeros((replicas * capacity, block_size), jnp.bfloat16).at[place_at]]
    convert_element_type x1 -> x0, other arithmetic: 8.55 us -> none  [per_device(): (cleared + weight_grad.reshape(block_count, block_size)).astype(jnp.bfloa...]
    reshape x2 -> x0, local copies, waits for them, and re-layouts: 7.37 us -> none  [the longest x1 6.48 us: per_device(): weight_grad.reshape(block_count, block_size)]
  transfers between devices with their start and end apart: 4 -> 10, of which waited for: 4 -> 3; matrix products, arithmetic and copies ran while one was open for 39% -> 8% of each run, Pallas kernels for 0% -> 21%
where the time goes in v1:
time: 75.6 us; the launch traced here: 74.9 us
  starting transfers between devices  25.7 us (34%)
  waiting for transfers between devices  20.5 us (27%)
  Pallas kernels  17.4 us (23%)
  local copies, waits for them, and re-layouts  6.55 us (9%)
  matrix products  3.81 us (5%)
  between operations  0.8 us (1%)
    ppermute x9, waiting for transfers between devices, shift(): return lax.ppermute(x, 'shard', [(i, (i + k) % n) for i in range(n)])  20.5 us
    ppermute x9, starting transfers between devices, shift(): return lax.ppermute(x, 'shard', [(i, (i + k) % n) for i in range(n)])  13.6 us
    all_to_all x1, starting transfers between devices, per_device(): got = lax.all_to_all(send, 'rep', split_axis=0, concat_axis=0, tiled=True)  12.1 us
    pallas_call x1, Pallas kernels, prep(): pl.pallas_call(prep_kernel, out_shape=(jax.ShapeDtypeStruct((owners, ROWS...  7.04 us
    pallas_call x1, Pallas kernels, grad_update(): pl.pallas_call(grad_kernel, out_shape=jax.ShapeDtypeStruct(cleared.shape,...  7 us
    unnamed x18, local copies, waits for them, and re-layouts  4.01 us
    dot_general x4, matrix products, nt_dot(): lax.dot_general(a, b, (((1,), (1,)), ((), ())), preferred_element_type=F32)  3.81 us
    dynamic_slice x1, local copies, waits for them, and re-layouts, per_device(): lax.dynamic_slice_in_dim(activ, lax.rem(my + k, shards) * width, width, a...  2.54 us
  transfers between devices with their start and end apart: 10, of which 3 were waited for; matrix products, arithmetic and copies ran while one was open for 8% of the time, Pallas kernels for 21%

profile of v1, /device:TPU:8, one launch (start us, length us, event | category | flops | bytes accessed | tf_op | source)
XLA Modules:
  0.0 74.9 jit_solution(12246866681775514404)
XLA Ops:
  0.6 0.0 copy-start
  0.6 0.0 copy-start.6
  0.7 0.0 copy-start.7
  0.7 2.8 %collective-permute-start = (bf16[128,640]{1,0:T(8,128)(2,1)}, bf16[128,640]{1,0:T(8,128)(2,1)S(1)}, u32[]{:S(2)}, u32[]{:S(2)}) collective-permute-start(bf16[128,640]{1,0:T(8,128)(2,1)} %g0.1), channel_id=1, source_target_pairs={{0,3},{1,0},{2,1},{3,2},{4,7},{5,4},{6,5},{7,6},{8,11},{9,8},{10,9... | collective-permute-start | bytes 491528 | tf_op jit(solution)/shard_map/ppermute | solution.py:200
  3.5 0.8 %collective-permute-start.2 = (bf16[128,640]{1,0:T(8,128)(2,1)}, bf16[128,640]{1,0:T(8,128)(2,1)S(1)}, u32[]{:S(2)}, u32[]{:S(2)}) collective-permute-start(bf16[128,640]{1,0:T(8,128)(2,1)} %g0.1), channel_id=1, source_target_pairs={{0,2},{1,3},{2,0},{3,1},{4,6},{5,7},{6,4},{7,5},{8,10},{9,11},{10,... | collective-permute-start | bytes 491528 | tf_op jit(solution)/shard_map/ppermute | solution.py:200
  4.3 0.9 %collective-permute-start.4 = (bf16[128,640]{1,0:T(8,128)(2,1)}, bf16[128,640]{1,0:T(8,128)(2,1)S(1)}, u32[]{:S(2)}, u32[]{:S(2)}) collective-permute-start(bf16[128,640]{1,0:T(8,128)(2,1)} %g0.1), channel_id=1, source_target_pairs={{0,1},{1,2},{2,3},{3,0},{4,5},{5,6},{6,7},{7,4},{8,9},{9,10},{10,1... | collective-permute-start | bytes 491528 | tf_op jit(solution)/shard_map/ppermute | solution.py:200
  5.2 2.5 %constant_dynamic-slice_fusion = (bf16[128,2048]{1,0:T(8,128)(2,1)}, bf16[128,2048]{1,0:T(8,128)(2,1)}, bf16[128,2048]{1,0:T(8,128)(2,1)}) fusion(bf16[128,8192]{1,0:T(8,128)(2,1)} %a0.1, s32[]{:T(128)S(6)} %select_n.11, s32[]{:T(128)S(6)} %select_n.10, s32[]{:T(128)S(6)} %select_n.9), kind=kLoop, calls=%fused_computation.4 | loop fusion | bytes 3145740 | tf_op jit(solution)/shard_map/dynamic_slice | solution.py:216
  7.7 1.8 %collective-permute-start.6 = (bf16[128,2048]{1,0:T(8,128)(2,1)}, bf16[128,2048]{1,0:T(8,128)(2,1)}, u32[]{:S(2)}, u32[]{:S(2)}) collective-permute-start(bf16[128,2048]{1,0:T(8,128)(2,1)} %get-tuple-element.9), channel_id=1, source_target_pairs={{0,1},{1,2},{2,3},{3,0},{4,5},{5,6},{6,7},{7,4},{8,9},{9,10},{10,1... | collective-permute-start | bytes 1572872 | tf_op jit(solution)/shard_map/ppermute | solution.py:200
  9.5 2.0 %collective-permute-start.7 = (bf16[128,2048]{1,0:T(8,128)(2,1)}, bf16[128,2048]{1,0:T(8,128)(2,1)}, u32[]{:S(2)}, u32[]{:S(2)}) collective-permute-start(bf16[128,2048]{1,0:T(8,128)(2,1)} %get-tuple-element.8), channel_id=1, source_target_pairs={{0,2},{1,3},{2,0},{3,1},{4,6},{5,7},{6,4},{7,5},{8,10},{9,11},{10,... | collective-permute-start | bytes 1572872 | tf_op jit(solution)/shard_map/ppermute | solution.py:200
  11.5 0.0 copy-done.6
  11.5 0.0 copy-done.7
  11.5 0.0 copy-start.4
  11.5 1.7 %copy-done.4 = bf16[1,10240,128]{2,1,0:T(8,128)(2,1)S(1)} copy-done((bf16[1,10240,128]{2,1,0:T(8,128)(2,1)S(1)}, bf16[1,10240,128]{2,1,0:T(8,128)(2,1)}, u32[]{:S(2)}) %copy-start.4) | copy-done | bytes 2621464
  13.3 7.0 %prep.1 = (bf16[64,24,128]{2,1,0:T(8,128)(2,1)}, bf16[10240,128]{1,0:T(8,128)(2,1)S(1)}) custom-call(s32[1]{0:T(128)} %bitcast.1.me_ref, s32[1,1,512]{2,1,0:T(1,128)S(1)} %copy-done.6, s32[1,64]{1,0:T(1,128)S(1)} %copy-done.7, bf16[10240,128]{1,0:T(8,128)(2,1)S(1)} %bitcast.13), custom_call_target="tpu_custom_call" | custom-call | flops 30000000 | bytes 5242880 | tf_op jit(solution)/shard_map/prep/pallas_call | solution.py:86
  20.3 0.0 copy-start.2
  20.3 1.5 %copy-done.2 = bf16[10240,128]{1,0:T(8,128)(2,1)} copy-done((bf16[10240,128]{1,0:T(8,128)(2,1)}, bf16[10240,128]{1,0:T(8,128)(2,1)S(1)}, u32[]{:S(2)}) %copy-start.2) | copy-done | bytes 2621464
  21.8 12.1 %all-to-all-start = ((bf16[64,24,128]{2,1,0:T(8,128)(2,1)}), bf16[64,24,128]{2,1,0:T(8,128)(2,1)S(1)}, u32[]{:S(2)}, u32[]{:S(2)}) async-start(bf16[64,24,128]{2,1,0:T(8,128)(2,1)} %get-tuple-element.6), calls=%async_computation | async-start | bytes 786432 | tf_op jit(solution)/shard_map/all_to_all | solution.py:223
  33.9 0.0 collective-permute-done.g3
  33.9 0.7 collective-permute-start.8
  34.7 0.0 copy-done
  34.7 0.9 %convolution_convert_fusion.2 = bf16[128,2048]{1,0:T(8,128)(2,1)S(1)} fusion(bf16[128,640]{1,0:T(8,128)(2,1)S(1)} %collective-permute-done.g3, bf16[2048,640]{1,0:T(8,128)(2,1)S(1)} %copy-done), kind=kOutput, calls=%fused_computation.2 | convolution fusion | flops 335806464 | bytes 3309568 | tf_op jit(solution)/shard_map/dot_general | solution.py:204
  35.6 0.0 copy-start.5
  35.7 0.0 collective-permute-done.2.g2
  35.7 1.4 %collective-permute-start.1 = (bf16[128,2048]{1,0:T(8,128)(2,1)S(1)}, bf16[128,2048]{1,0:T(8,128)(2,1)S(1)}, u32[]{:S(2)}, u32[]{:S(2)}) collective-permute-start(bf16[128,2048]{1,0:T(8,128)(2,1)S(1)} %convolution_convert_fusion.2), channel_id=1, source_target_pairs={{0,1},{1,2},{2,3},{3,0},{4,5},{5,6},{6,7},{7,4},{8,9},{9,10},{10,1... | collective-permute-start | bytes 1572872 | tf_op jit(solution)/shard_map/ppermute | solution.py:200
  37.1 0.9 %convolution_convert_fusion.1 = bf16[128,2048]{1,0:T(8,128)(2,1)S(1)} fusion(bf16[128,640]{1,0:T(8,128)(2,1)S(1)} %collective-permute-done.2.g2, bf16[2048,640]{1,0:T(8,128)(2,1)S(1)} %copy-done), kind=kOutput, calls=%fused_computation.1 | convolution fusion | flops 335806464 | bytes 3309568 | tf_op jit(solution)/shard_map/dot_general | solution.py:204
  38.1 0.0 copy-start.1
  38.1 0.0 copy-start.3
  38.1 0.0 collective-permute-done.4.g1
  38.1 1.6 %collective-permute-start.3 = (bf16[128,2048]{1,0:T(8,128)(2,1)S(1)}, bf16[128,2048]{1,0:T(8,128)(2,1)S(1)}, u32[]{:S(2)}, u32[]{:S(2)}) collective-permute-start(bf16[128,2048]{1,0:T(8,128)(2,1)S(1)} %convolution_convert_fusion.1), channel_id=1, source_target_pairs={{0,2},{1,3},{2,0},{3,1},{4,6},{5,7},{6,4},{7,5},{8,10},{9,11},{10,... | collective-permute-start | bytes 1572872 | tf_op jit(solution)/shard_map/ppermute | solution.py:200
  39.7 1.0 %convolution_convert_fusion = bf16[128,2048]{1,0:T(8,128)(2,1)S(1)} fusion(bf16[128,640]{1,0:T(8,128)(2,1)S(1)} %collective-permute-done.4.g1, bf16[2048,640]{1,0:T(8,128)(2,1)S(1)} %copy-done), kind=kOutput, calls=%fused_computation | convolution fusion | flops 335806464 | bytes 3309568 | tf_op jit(solution)/shard_map/dot_general | solution.py:204
  40.7 0.0 collective-permute-done.6.a1
  40.7 1.5 %collective-permute-start.5 = (bf16[128,2048]{1,0:T(8,128)(2,1)S(1)}, bf16[128,2048]{1,0:T(8,128)(2,1)S(1)}, u32[]{:S(2)}, u32[]{:S(2)}) collective-permute-start(bf16[128,2048]{1,0:T(8,128)(2,1)S(1)} %convolution_convert_fusion), channel_id=1, source_target_pairs={{0,3},{1,0},{2,1},{3,2},{4,7},{5,4},{6,5},{7,6},{8,11},{9,8},{10,9... | collective-permute-start | bytes 1572872 | tf_op jit(solution)/shard_map/ppermute | solution.py:200
  42.2 0.0 copy-done.5
  42.2 1.0 %convolution_convert_fusion.3.p0 = bf16[128,2048]{1,0:T(8,128)(2,1)S(1)} fusion(bf16[128,640]{1,0:T(8,128)(2,1)S(1)} %copy-done.5, bf16[2048,640]{1,0:T(8,128)(2,1)S(1)} %copy-done), kind=kOutput, calls=%fused_computation.3 | convolution fusion | flops 335806464 | bytes 3309568 | tf_op jit(solution)/shard_map/dot_general | solution.py:204
  43.2 0.0 collective-permute-done.7.a2
  43.2 5.9 %collective-permute-done.8.a3 = bf16[128,2048]{1,0:T(8,128)(2,1)S(1)} collective-permute-done((bf16[128,2048]{1,0:T(8,128)(2,1)}, bf16[128,2048]{1,0:T(8,128)(2,1)S(1)}, u32[]{:S(2)}, u32[]{:S(2)}) %collective-permute-start.8) | collective-permute-done | bytes 524320 | tf_op jit(solution)/shard_map/ppermute | solution.py:200
  49.0 0.0 copy-done.1
  49.0 0.0 copy-done.3
  49.0 7.0 %grad_update.1 = bf16[10240,128]{1,0:T(8,128)(2,1)} custom-call(s32[1]{0:T(128)} %bitcast.my_ref, bf16[128,8192]{1,0:T(8,128)(2,1)S(1)} %copy-done.1, bf16[128,2048]{1,0:T(8,128)(2,1)} %collective-permute-done.6.a1, bf16[128,2048]{1,0:T(8,128)(2,1)} %collective-permute-done.7.a2, bf16[128,2048]{1,0:T(8,128)(2,1)S(1)} %collective-permute-done.8.a3, ...), custom_call_target="tpu_custom_call" | custom-call | flops 1342177280 | bytes 12582912 | tf_op jit(solution)/shard_map/grad_update/pallas_call | solution.py:152
  56.0 5.8 %collective-permute-done.1.p1 = bf16[128,2048]{1,0:T(8,128)(2,1)S(1)} collective-permute-done((bf16[128,2048]{1,0:T(8,128)(2,1)S(1)}, bf16[128,2048]{1,0:T(8,128)(2,1)S(1)}, u32[]{:S(2)}, u32[]{:S(2)}) %collective-permute-start.1) | collective-permute-done | bytes 524320 | tf_op jit(solution)/shard_map/ppermute | solution.py:200
  61.9 0.0 collective-permute-done.3.p2
  61.9 8.8 %collective-permute-done.5.p3 = bf16[128,2048]{1,0:T(8,128)(2,1)S(1)} collective-permute-done((bf16[128,2048]{1,0:T(8,128)(2,1)S(1)}, bf16[128,2048]{1,0:T(8,128)(2,1)S(1)}, u32[]{:S(2)}, u32[]{:S(2)}) %collective-permute-start.5) | collective-permute-done | bytes 524320 | tf_op jit(solution)/shard_map/ppermute | solution.py:200
  70.7 1.3 %place.1 = bf16[128,8192]{1,0:T(8,128)(2,1)} custom-call(s32[1]{0:T(128)} %bitcast.my_ref, bf16[128,2048]{1,0:T(8,128)(2,1)S(1)} %convolution_convert_fusion.3.p0, bf16[128,2048]{1,0:T(8,128)(2,1)S(1)} %collective-permute-done.1.p1, bf16[128,2048]{1,0:T(8,128)(2,1)S(1)} %collective-permute-done.3.p2, bf16[128,2048]{1,0:T(8,128)(2,1)S(1)} %collective-permute-done.5.p3), custom_call_target="tpu_custom_call" | custom-call | flops 1000000 | bytes 4194304 | tf_op jit(solution)/shard_map/place/pallas_call | solution.py:187
  72.0 0.0 all-to-all-done.got_ref
  72.1 0.0 copy-start.8
  72.1 0.7 copy-done.8
  72.8 2.1 %owned.1 = f32[240,128]{1,0:T(8,128)} custom-call(bf16[64,24,128]{2,1,0:T(8,128)(2,1)} %copy-done.8), custom_call_target="tpu_custom_call" | custom-call | flops 4000000 | bytes 393216 | tf_op jit(solution)/shard_map/owned/pallas_call | solution.py:122
Async XLA Ops:
  0.6 34.1 %copy-start = (bf16[2048,640]{1,0:T(8,128)(2,1)S(1)}, bf16[2048,640]{1,0:T(8,128)(2,1)}, u32[]{:S(2)}) copy-start(bf16[2048,640]{1,0:T(8,128)(2,1)} %param.8) | copy-start | bytes 7864324
  0.6 10.9 %copy-start.6 = (s32[1,1,512]{2,1,0:T(1,128)S(1)}, s32[1,1,512]{2,1,0:T(1,128)}, u32[]{:S(2)}) copy-start(s32[1,1,512]{2,1,0:T(1,128)} %kept_ref.1) | copy-start | bytes 6148
  0.7 10.9 %copy-start.7 = (s32[1,64]{1,0:T(1,128)S(1)}, s32[1,64]{1,0:T(1,128)}, u32[]{:S(2)}) copy-start(s32[1,64]{1,0:T(1,128)} %len_ref.1) | copy-start | bytes 772
  0.7 33.3 %collective-permute-start = (bf16[128,640]{1,0:T(8,128)(2,1)}, bf16[128,640]{1,0:T(8,128)(2,1)S(1)}, u32[]{:S(2)}, u32[]{:S(2)}) collective-permute-start(bf16[128,640]{1,0:T(8,128)(2,1)} %g0.1), channel_id=1, source_target_pairs={{0,3},{1,0},{2,1},{3,2},{4,7},{5,4},{6,5},{7,6},{8,11},{9,8},{10,9... | collective-permute-start | bytes 491528 | tf_op jit(solution)/shard_map/ppermute | solution.py:200
  3.5 32.2 %collective-permute-start.2 = (bf16[128,640]{1,0:T(8,128)(2,1)}, bf16[128,640]{1,0:T(8,128)(2,1)S(1)}, u32[]{:S(2)}, u32[]{:S(2)}) collective-permute-start(bf16[128,640]{1,0:T(8,128)(2,1)} %g0.1), channel_id=1, source_target_pairs={{0,2},{1,3},{2,0},{3,1},{4,6},{5,7},{6,4},{7,5},{8,10},{9,11},{10,... | collective-permute-start | bytes 491528 | tf_op jit(solution)/shard_map/ppermute | solution.py:200
  4.3 33.8 %collective-permute-start.4 = (bf16[128,640]{1,0:T(8,128)(2,1)}, bf16[128,640]{1,0:T(8,128)(2,1)S(1)}, u32[]{:S(2)}, u32[]{:S(2)}) collective-permute-start(bf16[128,640]{1,0:T(8,128)(2,1)} %g0.1), channel_id=1, source_target_pairs={{0,1},{1,2},{2,3},{3,0},{4,5},{5,6},{6,7},{7,4},{8,9},{9,10},{10,1... | collective-permute-start | bytes 491528 | tf_op jit(solution)/shard_map/ppermute | solution.py:200
  7.7 32.9 %collective-permute-start.6 = (bf16[128,2048]{1,0:T(8,128)(2,1)}, bf16[128,2048]{1,0:T(8,128)(2,1)}, u32[]{:S(2)}, u32[]{:S(2)}) collective-permute-start(bf16[128,2048]{1,0:T(8,128)(2,1)} %get-tuple-element.9), channel_id=1, source_target_pairs={{0,1},{1,2},{2,3},{3,0},{4,5},{5,6},{6,7},{7,4},{8,9},{9,10},{10,1... | collective-permute-start | bytes 1572872 | tf_op jit(solution)/shard_map/ppermute | solution.py:200
  9.5 33.6 %collective-permute-start.7 = (bf16[128,2048]{1,0:T(8,128)(2,1)}, bf16[128,2048]{1,0:T(8,128)(2,1)}, u32[]{:S(2)}, u32[]{:S(2)}) collective-permute-start(bf16[128,2048]{1,0:T(8,128)(2,1)} %get-tuple-element.8), channel_id=1, source_target_pairs={{0,2},{1,3},{2,0},{3,1},{4,6},{5,7},{6,4},{7,5},{8,10},{9,11},{10,... | collective-permute-start | bytes 1572872 | tf_op jit(solution)/shard_map/ppermute | solution.py:200
  11.5 1.7 %copy-start.4 = (bf16[1,10240,128]{2,1,0:T(8,128)(2,1)S(1)}, bf16[1,10240,128]{2,1,0:T(8,128)(2,1)}, u32[]{:S(2)}) copy-start(bf16[1,10240,128]{2,1,0:T(8,128)(2,1)} %param.9) | copy-start | bytes 7864324
  20.3 1.5 %copy-start.2 = (bf16[10240,128]{1,0:T(8,128)(2,1)}, bf16[10240,128]{1,0:T(8,128)(2,1)S(1)}, u32[]{:S(2)}) copy-start(bf16[10240,128]{1,0:T(8,128)(2,1)S(1)} %get-tuple-element.5.clear_ref) | copy-start | bytes 7864324
  21.8 50.2 %all-to-all-start = ((bf16[64,24,128]{2,1,0:T(8,128)(2,1)}), bf16[64,24,128]{2,1,0:T(8,128)(2,1)S(1)}, u32[]{:S(2)}, u32[]{:S(2)}) async-start(bf16[64,24,128]{2,1,0:T(8,128)(2,1)} %get-tuple-element.6), calls=%async_computation | async-start | bytes 786432 | tf_op jit(solution)/shard_map/all_to_all | solution.py:223
  33.9 15.1 %collective-permute-start.8 = (bf16[128,2048]{1,0:T(8,128)(2,1)}, bf16[128,2048]{1,0:T(8,128)(2,1)S(1)}, u32[]{:S(2)}, u32[]{:S(2)}) collective-permute-start(bf16[128,2048]{1,0:T(8,128)(2,1)} %get-tuple-element.7), channel_id=1, source_target_pairs={{0,3},{1,0},{2,1},{3,2},{4,7},{5,4},{6,5},{7,6},{8,11},{9,8},{10,9... | collective-permute-start | bytes 1572872 | tf_op jit(solution)/shard_map/ppermute | solution.py:200
  35.6 6.5 %copy-start.5 = (bf16[128,640]{1,0:T(8,128)(2,1)S(1)}, bf16[128,640]{1,0:T(8,128)(2,1)}, u32[]{:S(2)}) copy-start(bf16[128,640]{1,0:T(8,128)(2,1)} %g0.1) | copy-start | bytes 491524
  35.7 26.2 %collective-permute-start.1 = (bf16[128,2048]{1,0:T(8,128)(2,1)S(1)}, bf16[128,2048]{1,0:T(8,128)(2,1)S(1)}, u32[]{:S(2)}, u32[]{:S(2)}) collective-permute-start(bf16[128,2048]{1,0:T(8,128)(2,1)S(1)} %convolution_convert_fusion.2), channel_id=1, source_target_pairs={{0,1},{1,2},{2,3},{3,0},{4,5},{5,6},{6,7},{7,4},{8,9},{9,10},{10,1... | collective-permute-start | bytes 1572872 | tf_op jit(solution)/shard_map/ppermute | solution.py:200
  38.1 11.0 %copy-start.1 = (bf16[128,8192]{1,0:T(8,128)(2,1)S(1)}, bf16[128,8192]{1,0:T(8,128)(2,1)}, u32[]{:S(2)}) copy-start(bf16[128,8192]{1,0:T(8,128)(2,1)} %a0.1) | copy-start | bytes 6291460
  38.1 11.0 %copy-start.3 = (bf16[10240,128]{1,0:T(8,128)(2,1)S(1)}, bf16[10240,128]{1,0:T(8,128)(2,1)}, u32[]{:S(2)}) copy-start(bf16[10240,128]{1,0:T(8,128)(2,1)} %copy-done.2) | copy-start | bytes 7864324
  38.1 23.8 %collective-permute-start.3 = (bf16[128,2048]{1,0:T(8,128)(2,1)S(1)}, bf16[128,2048]{1,0:T(8,128)(2,1)S(1)}, u32[]{:S(2)}, u32[]{:S(2)}) collective-permute-start(bf16[128,2048]{1,0:T(8,128)(2,1)S(1)} %convolution_convert_fusion.1), channel_id=1, source_target_pairs={{0,2},{1,3},{2,0},{3,1},{4,6},{5,7},{6,4},{7,5},{8,10},{9,11},{10,... | collective-permute-start | bytes 1572872 | tf_op jit(solution)/shard_map/ppermute | solution.py:200
  40.7 30.0 %collective-permute-start.5 = (bf16[128,2048]{1,0:T(8,128)(2,1)S(1)}, bf16[128,2048]{1,0:T(8,128)(2,1)S(1)}, u32[]{:S(2)}, u32[]{:S(2)}) collective-permute-start(bf16[128,2048]{1,0:T(8,128)(2,1)S(1)} %convolution_convert_fusion), channel_id=1, source_target_pairs={{0,3},{1,0},{2,1},{3,2},{4,7},{5,4},{6,5},{7,6},{8,11},{9,8},{10,9... | collective-permute-start | bytes 1572872 | tf_op jit(solution)/shard_map/ppermute | solution.py:200
  72.1 0.8 %copy-start.8 = (bf16[64,24,128]{2,1,0:T(8,128)(2,1)}, bf16[64,24,128]{2,1,0:T(8,128)(2,1)S(1)}, u32[]{:S(2)}) copy-start(bf16[64,24,128]{2,1,0:T(8,128)(2,1)S(1)} %all-to-all-done.got_ref) | copy-start | bytes 1179652

commit v2 on v1

--- a/solution.py
+++ b/solution.py
@@ -4,6 +4,7 @@
 from jax.experimental import pallas as pl
 from jax.experimental.pallas import tpu as pltpu
 from jax.sharding import PartitionSpec as P
+
 
 BF = jnp.bfloat16
 F32 = jnp.float32
@@ -15,17 +16,49 @@
 GROUP = 8
 
 
-def prep_kernel(me_ref, kept_ref, len_ref, table_ref, send_ref, clear_ref, wide, outbox, base, low, high, count):
-    blocks = table_ref.shape[0]
+def pack_kernel(my_ref, activ_ref, o1, o2, o3, sems):
+    width = o1.shape[1]
+    copies = []
+    for k, out in ((1, o1), (3, o3), (2, o2)):
+        column = lax.rem(my_ref[0] + k, 4) * width
+        copy = pltpu.make_async_copy(
+            activ_ref.at[:, pl.ds(pl.multiple_of(column, width), width)], out, sems.at[k - 1]
+        )
+        copy.start()
+        copies.append(copy)
+    for copy in copies:
+        copy.wait()
+
+
+def pack(my, activ, width):
+    piece = jax.ShapeDtypeStruct((activ.shape[0], width), BF)
+    return pl.pallas_call(
+        pack_kernel,
+        out_shape=(piece,) * 3,
+        in_specs=[pl.BlockSpec(memory_space=SMEM), pl.BlockSpec(memory_space=pltpu.HBM)],
+        out_specs=(pl.BlockSpec(memory_space=VMEM),) * 3,
+        scratch_shapes=[pltpu.SemaphoreType.DMA((3,))],
+        compiler_params=pltpu.CompilerParams(vmem_limit_bytes=59 << 20),
+        cost_estimate=pl.CostEstimate(flops=1_000_000, bytes_accessed=4 << 20, transcendentals=0),
+        name="pack",
+    )(my, activ)
+
+
+def prep_kernel(
+    me_ref, kept_ref, len_ref, table_ref, send_ref, clear_ref, held, wide, outbox, base, low, high, count, sems
+):
+    blocks = held.shape[0]
     owners = send_ref.shape[0]
-    chunk = 512
-
-    def widen(i, carry):
-        rows = pl.ds(pl.multiple_of(i * chunk, chunk), chunk)
-        wide[rows, :] = table_ref[rows, :].astype(F32)
-        return carry
-
-    lax.fori_loop(0, blocks // chunk, widen, 0)
+    parts = sems.shape[0]
+    part = blocks // parts
+    chunk = 256
+
+    def span(p):
+        return pl.ds(p * part, part)
+
+    loads = [pltpu.make_async_copy(table_ref.at[span(p)], held.at[span(p)], sems.at[p]) for p in range(parts)]
+    for load in loads:
+        load.start()
     outbox[...] = jnp.zeros_like(outbox)
 
     def reset(i, carry):
@@ -46,6 +79,15 @@
         return owner, first, last
 
     lax.fori_loop(0, blocks // BUCKET, tabulate, (jnp.int32(0), jnp.int32(0), len_ref[0, 0]), unroll=4)
+
+    def widen(i, carry):
+        rows = pl.ds(pl.multiple_of(i * chunk, chunk), chunk)
+        wide[rows, :] = held[rows, :].astype(F32)
+        return carry
+
+    for p, load in enumerate(loads):
+        load.wait()
+        lax.fori_loop(p * part // chunk, (p + 1) * part // chunk, widen, 0)
 
     lane = lax.broadcasted_iota(jnp.int32, (1, 128), 1)
     lane_base = lax.rem(me_ref[0], GROUP) * SLOTS
@@ -71,35 +113,45 @@
 
     def narrow(i, carry):
         rows = pl.ds(pl.multiple_of(i * chunk, chunk), chunk)
-        clear_ref[rows, :] = wide[rows, :].astype(BF)
+        held[rows, :] = wide[rows, :].astype(BF)
         return carry
 
-    lax.fori_loop(0, blocks // chunk, narrow, 0)
+    stores = []
+    for p in range(parts):
+        lax.fori_loop(p * part // chunk, (p + 1) * part // chunk, narrow, 0)
+        store = pltpu.make_async_copy(held.at[span(p)], clear_ref.at[span(p)], sems.at[p])
+        store.start()
+        stores.append(store)
     for o in range(owners):
         send_ref[o] = outbox[o * ROWS : (o + 1) * ROWS, :].astype(BF)
+    for store in stores:
+        store.wait()
 
 
 def prep(me, kept, lengths, table, owners):
     blocks, width = table.shape
     smem = pl.BlockSpec(memory_space=SMEM)
     vmem = pl.BlockSpec(memory_space=VMEM)
+    whole = pl.BlockSpec(memory_space=pltpu.HBM)
     return pl.pallas_call(
         prep_kernel,
         out_shape=(
             jax.ShapeDtypeStruct((owners, ROWS, width), BF),
             jax.ShapeDtypeStruct((blocks, width), BF),
         ),
-        in_specs=[smem, smem, smem, vmem],
-        out_specs=(vmem, vmem),
+        in_specs=[smem, smem, smem, whole],
+        out_specs=(vmem, whole),
         scratch_shapes=[
+            VMEM((blocks, width), BF),
             VMEM((blocks, width), F32),
             VMEM((owners * ROWS, width), F32),
             SMEM((blocks // BUCKET,), jnp.int32),
             SMEM((blocks // BUCKET,), jnp.int32),
             SMEM((blocks // BUCKET,), jnp.int32),
             SMEM((owners,), jnp.int32),
+            pltpu.SemaphoreType.DMA((4,)),
         ],
-        compiler_params=pltpu.CompilerParams(vmem_limit_bytes=24 << 20),
+        compiler_params=pltpu.CompilerParams(vmem_limit_bytes=58 << 20),
         cost_estimate=pl.CostEstimate(flops=30_000_000, bytes_accessed=4 * blocks * width, transcendentals=0),
         name="prep",
     )(me, kept, lengths, table)
@@ -124,6 +176,7 @@
         out_shape=jax.ShapeDtypeStruct((region_max, got.shape[2]), F32),
         in_specs=[pl.BlockSpec(memory_space=VMEM)],
         out_specs=pl.BlockSpec(memory_space=VMEM),
+        compiler_params=pltpu.CompilerParams(vmem_limit_bytes=4 << 20),
         cost_estimate=pl.CostEstimate(flops=4_000_000, bytes_accessed=got.size * 2, transcendentals=0),
         name="owned",
     )(got)
@@ -160,7 +213,7 @@
             out_specs=rows,
             scratch_shapes=[VMEM((tile * per, 128), F32)],
         ),
-        compiler_params=pltpu.CompilerParams(vmem_limit_bytes=24 << 20),
+        compiler_params=pltpu.CompilerParams(vmem_limit_bytes=58 << 20),
         cost_estimate=pl.CostEstimate(
             flops=2 * 4 * tokens * features * keys, bytes_accessed=12 << 20, transcendentals=0
         ),
@@ -204,36 +257,46 @@
     return lax.dot_general(a, b, (((1,), (1,)), ((), ())), preferred_element_type=F32).astype(BF)
 
 
-def per_device(activ, key_grad, key_weight, feedback, kept, region_len):
+def after(x, *earlier):
+    return lax.optimization_barrier((x, *earlier))[0]
+
+
+def step(activ, key_grad, key_weight, feedback, kept, region_len):
     shards = lax.axis_size("shard")
     my = lax.axis_index("shard")
     me = lax.axis_index("rep").reshape(1)
     my1 = my.reshape(1)
     owners = lax.axis_size("rep")
     width = activ.shape[1] // shards
-    kgs = {k: shift(key_grad, k) for k in (1, 3, 2)}
-    outgoing = {
-        k: lax.dynamic_slice_in_dim(activ, lax.rem(my + k, shards) * width, width, axis=1) for k in (1, 3, 2)
-    }
-    acts = {k: shift(outgoing[k], k) for k in (1, 3, 2)}
+    order = (1, 3, 2)
+    kgs, acts, parts, back = {}, {}, {}, {}
+    for k in order:
+        kgs[k] = shift(key_grad, k)
+    outgoing = dict(zip((1, 2, 3), pack(my1, activ, width)))
+    for k in order:
+        acts[k] = shift(outgoing[k], k)
     table = feedback[0]
     blocks = table.shape[0]
     mean_len = blocks // owners
     send, cleared = prep(me, kept, region_len, table, owners)
+    for k in order:
+        parts[k] = nt_dot(kgs[k], key_weight)
+        back[k] = shift(parts[k], shards - k)
+    own_part = nt_dot(key_grad, key_weight)
+    send = after(send, own_part)
     got = lax.all_to_all(send, "rep", split_axis=0, concat_axis=0, tiled=True)
-    own_part = nt_dot(key_grad, key_weight)
-    back = {k: shift(nt_dot(kgs[k], key_weight), shards - k) for k in (1, 3, 2)}
     updated = grad_update(
         my1, activ, [acts[1], acts[2], acts[3]], [key_grad, kgs[1], kgs[2], kgs[3]], cleared
     )
     owned_rows = owned(got, mean_len + mean_len // 2)
-    input_grad = place(my1, [own_part, back[3], back[2], back[1]])
+    pieces = lax.optimization_barrier(([own_part, back[3], back[2], back[1]], owned_rows))[0]
+    input_grad = place(my1, pieces)
     return (input_grad, updated[None], owned_rows[None])
 
 
 def solution(mesh):
     return jax.shard_map(
-        per_device,
+        step,
         mesh=mesh,
         in_specs=(
             P(("rep", "shard"), None),

time: 75.6 us -> 74.2 us (0.981)
  waiting for transfers between devices: 20.5 us -> 13.2 us
  local copies, waits for them, and re-layouts: 6.55 us -> 0.82 us
  Pallas kernels: 17.4 us -> 23.1 us
  matrix products: 3.81 us -> 8.94 us
  starting transfers between devices: 25.7 us -> 26.8 us
    ppermute x9, waiting for transfers between devices: 20.5 us -> 13.2 us  [shift(): return lax.ppermute(x, 'shard', [(i, (i + k) % n) for i in range(n)])]
    dot_general x4, matrix products: 3.81 us -> 8.94 us  [nt_dot(): lax.dot_general(a, b, (((1,), (1,)), ((), ())), preferred_element_type=F32)]
    unnamed x18 -> x6, local copies, waits for them, and re-layouts: 4.01 us -> 0.82 us
    dynamic_slice x1 -> x0, local copies, waits for them, and re-layouts: 2.54 us -> none  [per_device(): lax.dynamic_slice_in_dim(activ, lax.rem(my + k, shards) * width, width, a...]
    pallas_call x0 -> x1, Pallas kernels: none -> 2.52 us  [pack(): pl.pallas_call(pack_kernel, out_shape=(piece,) * 3, in_specs=[pl.BlockSpe...]
    pallas_call x1, Pallas kernels: 7.04 us -> 8.7 us  [prep(): pl.pallas_call(prep_kernel, out_shape=(jax.ShapeDtypeStruct((owners, ROWS...]
    pallas_call x1, Pallas kernels: 1.34 us -> 2.7 us  [place(): pl.pallas_call(place_kernel, out_shape=jax.ShapeDtypeStruct((tokens, 4 *...]
    pallas_call x1, Pallas kernels: 7 us -> 8.1 us  [grad_update(): pl.pallas_call(grad_kernel, out_shape=jax.ShapeDtypeStruct(cleared.shape,...]
  transfers between devices with their start and end apart: 10 -> 10, of which waited for: 3 -> 3; matrix products, arithmetic and copies ran while one was open for 8% -> 12% of each run, Pallas kernels for 21% -> 28%
where the time goes in v2:
time: 74.2 us; the launch traced here: 73.6 us
  starting transfers between devices  26.8 us (36%)
  Pallas kernels  23.1 us (31%)
  waiting for transfers between devices  13.2 us (18%)
  matrix products  8.94 us (12%)
  local copies, waits for them, and re-layouts  0.82 us (1%)
    ppermute x9, starting transfers between devices, shift(): return lax.ppermute(x, 'shard', [(i, (i + k) % n) for i in range(n)])  14.7 us
    ppermute x9, waiting for transfers between devices, shift(): return lax.ppermute(x, 'shard', [(i, (i + k) % n) for i in range(n)])  13.2 us
    all_to_all x1, starting transfers between devices, step(): got = lax.all_to_all(send, 'rep', split_axis=0, concat_axis=0, tiled=True)  12.1 us
    dot_general x4, matrix products, nt_dot(): lax.dot_general(a, b, (((1,), (1,)), ((), ())), preferred_element_type=F32)  8.94 us
    pallas_call x1, Pallas kernels, prep(): pl.pallas_call(prep_kernel, out_shape=(jax.ShapeDtypeStruct((owners, ROWS...  8.7 us
    pallas_call x1, Pallas kernels, grad_update(): pl.pallas_call(grad_kernel, out_shape=jax.ShapeDtypeStruct(cleared.shape,...  8.1 us
    pallas_call x1, Pallas kernels, place(): pl.pallas_call(place_kernel, out_shape=jax.ShapeDtypeStruct((tokens, 4 *...  2.7 us
    pallas_call x1, Pallas kernels, pack(): pl.pallas_call(pack_kernel, out_shape=(piece,) * 3, in_specs=[pl.BlockSpe...  2.52 us
  transfers between devices with their start and end apart: 10, of which 3 were waited for; matrix products, arithmetic and copies ran while one was open for 12% of the time, Pallas kernels for 28%

profile of v2, /device:TPU:8, one launch (start us, length us, event | category | flops | bytes accessed | tf_op | source)
XLA Modules:
  0.0 73.6 jit_solution(9833500468787739356)
XLA Ops:
  0.6 0.0 copy-start
  0.6 0.0 copy-start.1
  0.7 3.1 %collective-permute-start.2 = (bf16[128,640]{1,0:T(8,128)(2,1)}, bf16[128,640]{1,0:T(8,128)(2,1)}, u32[]{:S(2)}, u32[]{:S(2)}) collective-permute-start(bf16[128,640]{1,0:T(8,128)(2,1)} %g0.1), channel_id=1, source_target_pairs={{0,2},{1,3},{2,0},{3,1},{4,6},{5,7},{6,4},{7,5},{8,10},{9,11},{10,... | collective-permute-start | bytes 491528 | tf_op jit(solution)/shard_map/ppermute | solution.py:253
  3.8 1.1 %collective-permute-start = (bf16[128,640]{1,0:T(8,128)(2,1)}, bf16[128,640]{1,0:T(8,128)(2,1)}, u32[]{:S(2)}, u32[]{:S(2)}) collective-permute-start(bf16[128,640]{1,0:T(8,128)(2,1)} %g0.1), channel_id=1, source_target_pairs={{0,3},{1,0},{2,1},{3,2},{4,7},{5,4},{6,5},{7,6},{8,11},{9,8},{10,9... | collective-permute-start | bytes 491528 | tf_op jit(solution)/shard_map/ppermute | solution.py:253
  4.9 0.9 %collective-permute-start.4 = (bf16[128,640]{1,0:T(8,128)(2,1)}, bf16[128,640]{1,0:T(8,128)(2,1)}, u32[]{:S(2)}, u32[]{:S(2)}) collective-permute-start(bf16[128,640]{1,0:T(8,128)(2,1)} %g0.1), channel_id=1, source_target_pairs={{0,1},{1,2},{2,3},{3,0},{4,5},{5,6},{6,7},{7,4},{8,9},{9,10},{10,1... | collective-permute-start | bytes 491528 | tf_op jit(solution)/shard_map/ppermute | solution.py:253
  5.8 2.5 %pack.1 = (bf16[128,2048]{1,0:T(8,128)(2,1)}, bf16[128,2048]{1,0:T(8,128)(2,1)}, bf16[128,2048]{1,0:T(8,128)(2,1)}) custom-call(s32[1]{0:T(128)} %bitcast.my_ref, bf16[128,8192]{1,0:T(8,128)(2,1)} %a0.1), custom_call_target="tpu_custom_call" | custom-call | flops 1000000 | bytes 4194304 | tf_op jit(solution)/shard_map/pack/pallas_call | solution.py:35
  8.3 0.7 collective-permute-start.6
  9.0 3.2 %collective-permute-start.7 = (bf16[128,2048]{1,0:T(8,128)(2,1)}, bf16[128,2048]{1,0:T(8,128)(2,1)}, u32[]{:S(2)}, u32[]{:S(2)}) collective-permute-start(bf16[128,2048]{1,0:T(8,128)(2,1)} %get-tuple-element.20), channel_id=1, source_target_pairs={{0,2},{1,3},{2,0},{3,1},{4,6},{5,7},{6,4},{7,5},{8,10},{9,11},{10,... | collective-permute-start | bytes 1572872 | tf_op jit(solution)/shard_map/ppermute | solution.py:253
  12.2 8.7 %prep.1 = (bf16[64,24,128]{2,1,0:T(8,128)(2,1)}, bf16[10240,128]{1,0:T(8,128)(2,1)}) custom-call(s32[1]{0:T(128)} %bitcast.1.me_ref, s32[1,1,512]{2,1,0:T(1,128)} %kept_ref.1, s32[1,64]{1,0:T(1,128)} %len_ref.1, bf16[10240,128]{1,0:T(8,128)(2,1)} %bitcast.14), custom_call_target="tpu_custom_call" | custom-call | flops 30000000 | bytes 5242880 | tf_op jit(solution)/shard_map/prep/pallas_call | solution.py:136
  20.9 0.0 copy-done
  20.9 0.0 copy-done.1
  20.9 0.9 %convolution_convert_fusion.3.p0 = bf16[128,2048]{1,0:T(8,128)(2,1)S(1)} fusion(bf16[128,640]{1,0:T(8,128)(2,1)S(1)} %copy-done.1, bf16[2048,640]{1,0:T(8,128)(2,1)S(1)} %copy-done), kind=kOutput, calls=%fused_computation.3 | convolution fusion | flops 335806464 | bytes 3309568 | tf_op jit(solution)/shard_map/dot_general | solution.py:257
  21.9 12.1 %all-to-all-start = ((bf16[64,24,128]{2,1,0:T(8,128)(2,1)}), bf16[64,24,128]{2,1,0:T(8,128)(2,1)S(1)}, u32[]{:S(2)}, u32[]{:S(2)}) async-start(bf16[64,24,128]{2,1,0:T(8,128)(2,1)} %get-tuple-element.14), calls=%async_computation | async-start | bytes 786432 | tf_op jit(solution)/shard_map/all_to_all | solution.py:287
  34.0 0.0 collective-permute-done.2.g2
  34.0 0.1 collective-permute-start.8
  34.1 2.7 %convolution_convert_fusion.1 = bf16[128,2048]{1,0:T(8,128)(2,1)} fusion(bf16[128,640]{1,0:T(8,128)(2,1)} %collective-permute-done.2.g2, bf16[2048,640]{1,0:T(8,128)(2,1)S(1)} %copy-done), kind=kOutput, calls=%fused_computation.1 | convolution fusion | flops 335806464 | bytes 3309568 | tf_op jit(solution)/shard_map/dot_general | solution.py:257
  36.8 0.0 collective-permute-done.g3
  36.8 2.3 %collective-permute-start.3 = (bf16[128,2048]{1,0:T(8,128)(2,1)}, bf16[128,2048]{1,0:T(8,128)(2,1)}, u32[]{:S(2)}, u32[]{:S(2)}) collective-permute-start(bf16[128,2048]{1,0:T(8,128)(2,1)} %convolution_convert_fusion.1), channel_id=1, source_target_pairs={{0,2},{1,3},{2,0},{3,1},{4,6},{5,7},{6,4},{7,5},{8,10},{9,11},{10,... | collective-permute-start | bytes 1572872 | tf_op jit(solution)/shard_map/ppermute | solution.py:253
  39.1 2.7 %convolution_convert_fusion.2 = bf16[128,2048]{1,0:T(8,128)(2,1)} fusion(bf16[128,640]{1,0:T(8,128)(2,1)} %collective-permute-done.g3, bf16[2048,640]{1,0:T(8,128)(2,1)S(1)} %copy-done), kind=kOutput, calls=%fused_computation.2 | convolution fusion | flops 335806464 | bytes 3309568 | tf_op jit(solution)/shard_map/dot_general | solution.py:257
  41.8 0.0 collective-permute-done.4.g1
  41.8 0.0 collective-permute-start.1
  41.8 2.7 %convolution_convert_fusion = bf16[128,2048]{1,0:T(8,128)(2,1)} fusion(bf16[128,640]{1,0:T(8,128)(2,1)} %collective-permute-done.4.g1, bf16[2048,640]{1,0:T(8,128)(2,1)S(1)} %copy-done), kind=kOutput, calls=%fused_computation | convolution fusion | flops 335806464 | bytes 3309568 | tf_op jit(solution)/shard_map/dot_general | solution.py:257
  44.5 0.0 collective-permute-done.6.a1
  44.5 3.2 %collective-permute-start.5 = (bf16[128,2048]{1,0:T(8,128)(2,1)}, bf16[128,2048]{1,0:T(8,128)(2,1)}, u32[]{:S(2)}, u32[]{:S(2)}) collective-permute-start(bf16[128,2048]{1,0:T(8,128)(2,1)} %convolution_convert_fusion), channel_id=1, source_target_pairs={{0,3},{1,0},{2,1},{3,2},{4,7},{5,4},{6,5},{7,6},{8,11},{9,8},{10,9... | collective-permute-start | bytes 1572872 | tf_op jit(solution)/shard_map/ppermute | solution.py:253
  47.7 0.0 collective-permute-done.7.a2
  47.7 1.4 %collective-permute-done.8.a3 = bf16[128,2048]{1,0:T(8,128)(2,1)S(1)} collective-permute-done((bf16[128,2048]{1,0:T(8,128)(2,1)}, bf16[128,2048]{1,0:T(8,128)(2,1)S(1)}, u32[]{:S(2)}, u32[]{:S(2)}) %collective-permute-start.8) | collective-permute-done | bytes 524320 | tf_op jit(solution)/shard_map/ppermute | solution.py:253
  49.1 0.0 copy-start.2
  49.1 0.8 %copy-done.2 = bf16[128,2048]{1,0:T(8,128)(2,1)} copy-done((bf16[128,2048]{1,0:T(8,128)(2,1)}, bf16[128,2048]{1,0:T(8,128)(2,1)S(1)}, u32[]{:S(2)}) %copy-start.2) | copy-done | bytes 524312
  49.9 8.1 %grad_update.1 = bf16[10240,128]{1,0:T(8,128)(2,1)} custom-call(s32[1]{0:T(128)} %bitcast.my_ref, bf16[128,8192]{1,0:T(8,128)(2,1)} %a0.1, bf16[128,2048]{1,0:T(8,128)(2,1)} %collective-permute-done.6.a1, bf16[128,2048]{1,0:T(8,128)(2,1)} %collective-permute-done.7.a2, bf16[128,2048]{1,0:T(8,128)(2,1)} %copy-done.2, bf16[128,640]{1,0:T(8,128)(2,1)} %g0.1, ...), custom_call_target="tpu_custom_call" | custom-call | flops 1342177280 | bytes 12582912 | tf_op jit(solution)/shard_map/grad_update/pallas_call | solution.py:205
  58.0 0.0 all-to-all-done.got_ref
  58.0 1.1 %owned.1 = f32[240,128]{1,0:T(8,128)} custom-call(bf16[64,24,128]{2,1,0:T(8,128)(2,1)S(1)} %all-to-all-done.got_ref), custom_call_target="tpu_custom_call" | custom-call | flops 4000000 | bytes 393216 | tf_op jit(solution)/shard_map/owned/pallas_call | solution.py:174
  59.1 0.0 collective-permute-done.3.p2
  59.1 4.7 %collective-permute-done.1.p1 = bf16[128,2048]{1,0:T(8,128)(2,1)} collective-permute-done((bf16[128,2048]{1,0:T(8,128)(2,1)}, bf16[128,2048]{1,0:T(8,128)(2,1)}, u32[]{:S(2)}, u32[]{:S(2)}) %collective-permute-start.1) | collective-permute-done | bytes 524320 | tf_op jit(solution)/shard_map/ppermute | solution.py:253
  63.8 7.1 %collective-permute-done.5.p3 = bf16[128,2048]{1,0:T(8,128)(2,1)} collective-permute-done((bf16[128,2048]{1,0:T(8,128)(2,1)}, bf16[128,2048]{1,0:T(8,128)(2,1)}, u32[]{:S(2)}, u32[]{:S(2)}) %collective-permute-start.5) | collective-permute-done | bytes 524320 | tf_op jit(solution)/shard_map/ppermute | solution.py:253
  70.9 2.7 %place.1 = bf16[128,8192]{1,0:T(8,128)(2,1)} custom-call(s32[1]{0:T(128)} %bitcast.my_ref, bf16[128,2048]{1,0:T(8,128)(2,1)S(1)} %convolution_convert_fusion.3.p0, bf16[128,2048]{1,0:T(8,128)(2,1)} %collective-permute-done.1.p1, bf16[128,2048]{1,0:T(8,128)(2,1)} %collective-permute-done.3.p2, bf16[128,2048]{1,0:T(8,128)(2,1)} %collective-permute-done.5.p3), custom_call_target="tpu_custom_call" | custom-call | flops 1000000 | bytes 4194304 | tf_op jit(solution)/shard_map/place/pallas_call | solution.py:240
Async XLA Ops:
  0.6 20.3 %copy-start = (bf16[2048,640]{1,0:T(8,128)(2,1)S(1)}, bf16[2048,640]{1,0:T(8,128)(2,1)}, u32[]{:S(2)}) copy-start(bf16[2048,640]{1,0:T(8,128)(2,1)} %param.8) | copy-start | bytes 7864324
  0.6 20.3 %copy-start.1 = (bf16[128,640]{1,0:T(8,128)(2,1)S(1)}, bf16[128,640]{1,0:T(8,128)(2,1)}, u32[]{:S(2)}) copy-start(bf16[128,640]{1,0:T(8,128)(2,1)} %g0.1) | copy-start | bytes 491524
  0.7 33.4 %collective-permute-start.2 = (bf16[128,640]{1,0:T(8,128)(2,1)}, bf16[128,640]{1,0:T(8,128)(2,1)}, u32[]{:S(2)}, u32[]{:S(2)}) collective-permute-start(bf16[128,640]{1,0:T(8,128)(2,1)} %g0.1), channel_id=1, source_target_pairs={{0,2},{1,3},{2,0},{3,1},{4,6},{5,7},{6,4},{7,5},{8,10},{9,11},{10,... | collective-permute-start | bytes 491528 | tf_op jit(solution)/shard_map/ppermute | solution.py:253
  3.8 33.0 %collective-permute-start = (bf16[128,640]{1,0:T(8,128)(2,1)}, bf16[128,640]{1,0:T(8,128)(2,1)}, u32[]{:S(2)}, u32[]{:S(2)}) collective-permute-start(bf16[128,640]{1,0:T(8,128)(2,1)} %g0.1), channel_id=1, source_target_pairs={{0,3},{1,0},{2,1},{3,2},{4,7},{5,4},{6,5},{7,6},{8,11},{9,8},{10,9... | collective-permute-start | bytes 491528 | tf_op jit(solution)/shard_map/ppermute | solution.py:253
  4.9 36.9 %collective-permute-start.4 = (bf16[128,640]{1,0:T(8,128)(2,1)}, bf16[128,640]{1,0:T(8,128)(2,1)}, u32[]{:S(2)}, u32[]{:S(2)}) collective-permute-start(bf16[128,640]{1,0:T(8,128)(2,1)} %g0.1), channel_id=1, source_target_pairs={{0,1},{1,2},{2,3},{3,0},{4,5},{5,6},{6,7},{7,4},{8,9},{9,10},{10,1... | collective-permute-start | bytes 491528 | tf_op jit(solution)/shard_map/ppermute | solution.py:253
  8.3 36.1 %collective-permute-start.6 = (bf16[128,2048]{1,0:T(8,128)(2,1)}, bf16[128,2048]{1,0:T(8,128)(2,1)}, u32[]{:S(2)}, u32[]{:S(2)}) collective-permute-start(bf16[128,2048]{1,0:T(8,128)(2,1)} %get-tuple-element.19), channel_id=1, source_target_pairs={{0,1},{1,2},{2,3},{3,0},{4,5},{5,6},{6,7},{7,4},{8,9},{9,10},{10,1... | collective-permute-start | bytes 1572872 | tf_op jit(solution)/shard_map/ppermute | solution.py:253
  9.0 38.7 %collective-permute-start.7 = (bf16[128,2048]{1,0:T(8,128)(2,1)}, bf16[128,2048]{1,0:T(8,128)(2,1)}, u32[]{:S(2)}, u32[]{:S(2)}) collective-permute-start(bf16[128,2048]{1,0:T(8,128)(2,1)} %get-tuple-element.20), channel_id=1, source_target_pairs={{0,2},{1,3},{2,0},{3,1},{4,6},{5,7},{6,4},{7,5},{8,10},{9,11},{10,... | collective-permute-start | bytes 1572872 | tf_op jit(solution)/shard_map/ppermute | solution.py:253
  21.9 36.1 %all-to-all-start = ((bf16[64,24,128]{2,1,0:T(8,128)(2,1)}), bf16[64,24,128]{2,1,0:T(8,128)(2,1)S(1)}, u32[]{:S(2)}, u32[]{:S(2)}) async-start(bf16[64,24,128]{2,1,0:T(8,128)(2,1)} %get-tuple-element.14), calls=%async_computation | async-start | bytes 786432 | tf_op jit(solution)/shard_map/all_to_all | solution.py:287
  34.0 15.1 %collective-permute-start.8 = (bf16[128,2048]{1,0:T(8,128)(2,1)}, bf16[128,2048]{1,0:T(8,128)(2,1)S(1)}, u32[]{:S(2)}, u32[]{:S(2)}) collective-permute-start(bf16[128,2048]{1,0:T(8,128)(2,1)} %get-tuple-element.21), channel_id=1, source_target_pairs={{0,3},{1,0},{2,1},{3,2},{4,7},{5,4},{6,5},{7,6},{8,11},{9,8},{10,9... | collective-permute-start | bytes 1572872 | tf_op jit(solution)/shard_map/ppermute | solution.py:253
  36.8 22.3 %collective-permute-start.3 = (bf16[128,2048]{1,0:T(8,128)(2,1)}, bf16[128,2048]{1,0:T(8,128)(2,1)}, u32[]{:S(2)}, u32[]{:S(2)}) collective-permute-start(bf16[128,2048]{1,0:T(8,128)(2,1)} %convolution_convert_fusion.1), channel_id=1, source_target_pairs={{0,2},{1,3},{2,0},{3,1},{4,6},{5,7},{6,4},{7,5},{8,10},{9,11},{10,... | collective-permute-start | bytes 1572872 | tf_op jit(solution)/shard_map/ppermute | solution.py:253
  41.8 22.0 %collective-permute-start.1 = (bf16[128,2048]{1,0:T(8,128)(2,1)}, bf16[128,2048]{1,0:T(8,128)(2,1)}, u32[]{:S(2)}, u32[]{:S(2)}) collective-permute-start(bf16[128,2048]{1,0:T(8,128)(2,1)} %convolution_convert_fusion.2), channel_id=1, source_target_pairs={{0,1},{1,2},{2,3},{3,0},{4,5},{5,6},{6,7},{7,4},{8,9},{9,10},{10,1... | collective-permute-start | bytes 1572872 | tf_op jit(solution)/shard_map/ppermute | solution.py:253
  44.5 26.4 %collective-permute-start.5 = (bf16[128,2048]{1,0:T(8,128)(2,1)}, bf16[128,2048]{1,0:T(8,128)(2,1)}, u32[]{:S(2)}, u32[]{:S(2)}) collective-permute-start(bf16[128,2048]{1,0:T(8,128)(2,1)} %convolution_convert_fusion), channel_id=1, source_target_pairs={{0,3},{1,0},{2,1},{3,2},{4,7},{5,4},{6,5},{7,6},{8,11},{9,8},{10,9... | collective-permute-start | bytes 1572872 | tf_op jit(solution)/shard_map/ppermute | solution.py:253
  49.1 0.8 %copy-start.2 = (bf16[128,2048]{1,0:T(8,128)(2,1)}, bf16[128,2048]{1,0:T(8,128)(2,1)S(1)}, u32[]{:S(2)}) copy-start(bf16[128,2048]{1,0:T(8,128)(2,1)S(1)} %collective-permute-done.8.a3) | copy-start | bytes 1572868

commit v3 on v2

v3 whole, which is shorter than its diff:
```python
import jax
import jax.numpy as jnp
from jax import lax
from jax.experimental import pallas as pl
from jax.experimental.pallas import tpu as pltpu
from jax.sharding import PartitionSpec as P


BF = jnp.bfloat16
F32 = jnp.float32
VMEM = pltpu.VMEM
SMEM = pltpu.SMEM
SLOTS = 16
ROWS = 24
GROUP = 8
TILE = 1024
PACK_LIMIT = 59
PREP_LIMIT = 58
GRAD_LIMIT = 50
DOTS_LIMIT = 40
DOTS_TILE = 1024


def bundle_copies(my, k, activ_ref, grad_ref, out, sems):
    keys = grad_ref.shape[1]
    width = out.shape[1] - keys
    column = pl.multiple_of(lax.rem(my + k, 4) * width, width)
    return [
        pltpu.make_async_copy(activ_ref.at[:, pl.ds(column, width)], out.at[:, keys:], sems.at[0]),
        pltpu.make_async_copy(grad_ref, out.at[:, :keys], sems.at[1]),
    ]


def pack_kernel(my_ref, index_ref, activ_ref, weight_ref, o1, o3, cut, sems):
    piece = cut.shape[0]
    first = pl.multiple_of(index_ref[0] * piece, piece)
    width = o1.shape[1]
    copies = [pltpu.make_async_copy(weight_ref.at[pl.ds(first, piece)], cut, sems.at[0])]
    for k, out in ((1, o1), (3, o3)):
        column = pl.multiple_of(lax.rem(my_ref[0] + k, 4) * width, width)
        copies.append(pltpu.make_async_copy(activ_ref.at[:, pl.ds(column, width)], out, sems.at[(k + 1) // 2]))
    for copy in copies:
        copy.start()
    for copy in copies:
        copy.wait()


def pack(my, index, activ, key_weight, width, piece):
    bundle = jax.ShapeDtypeStruct((activ.shape[0], width), BF)
    hbm = pl.BlockSpec(memory_space=pltpu.HBM)
    smem = pl.BlockSpec(memory_space=SMEM)
    return pl.pallas_call(
        pack_kernel,
        out_shape=(bundle, bundle, jax.ShapeDtypeStruct((piece, key_weight.shape[1]), BF)),
        in_specs=[smem, smem, hbm, hbm],
        out_specs=(pl.BlockSpec(memory_space=VMEM),) * 3,
        scratch_shapes=[pltpu.SemaphoreType.DMA((3,))],
        compiler_params=pltpu.CompilerParams(vmem_limit_bytes=PACK_LIMIT << 20),
        cost_estimate=pl.CostEstimate(flops=1_000_000, bytes_accessed=3 << 20, transcendentals=0),
        name="pack",
    )(my, index, activ, key_weight)


def nt(a, b):
    return lax.dot_general(a, b, (((1,), (1,)), ((), ())), preferred_element_type=F32)


def iota(shape, dim):
    return lax.broadcasted_iota(jnp.int32, shape, dim)


def bits(mask):
    return mask.astype(F32).astype(BF)


def prep_kernel(
    me_ref, my_ref, kept_ref, ids_ref, len_ref, table_ref, activ_ref, grad_ref,
    send_ref, mask_ref, o2, held, wide, outbox, spot_v, spot_s, sems, spot_sem, pack_sems
):
    blocks = held.shape[0]
    owners = send_ref.shape[0]
    keep = ids_ref.shape[2]
    parts = sems.shape[0]
    part = blocks // parts
    chunk = 256

    def span(p):
        return pl.ds(p * part, part)

    loads = [pltpu.make_async_copy(table_ref.at[span(p)], held.at[span(p)], sems.at[p]) for p in range(parts)]
    for load in loads:
        load.start()
    packs = bundle_copies(my_ref[0], 2, activ_ref, grad_ref, o2, pack_sems)
    for copy in packs:
        copy.start()

    ids = ids_ref[0]
    lengths = len_ref[...]
    starts = jnp.sum(
        jnp.where(iota((owners, owners), 1) < iota((owners, owners), 0), lengths, 0), axis=1, keepdims=True
    )
    ends = jnp.sum(
        jnp.where(iota((owners, owners), 1) <= iota((owners, owners), 0), lengths, 0), axis=1, keepdims=True
    )
    inside = ((ids >= starts) & (ids < ends)).astype(F32)
    before = bits(iota((keep, keep), 1) > iota((keep, keep), 0))
    earlier = lax.dot_general(inside.astype(BF), before, (((1,), (0,)), ((), ())), preferred_element_type=F32)
    slot = jnp.sum(inside * earlier, axis=0, keepdims=True)
    owner = jnp.sum(inside * iota((owners, 1), 0).astype(F32), axis=0, keepdims=True)
    offset = ids.astype(F32) - jnp.sum(inside * starts.astype(F32), axis=0, keepdims=True)
    spot_v[...] = (owner * ROWS + slot).astype(jnp.int32)
    fetch = pltpu.make_async_copy(spot_v, spot_s, spot_sem)
    fetch.start()
    lane_base = lax.rem(me_ref[0], GROUP) * SLOTS
    lane = bits(iota((128, keep), 0) == slot.astype(jnp.int32) + lane_base)
    tags = nt((inside * (offset + 1.0)).astype(BF), lane)
    high = lax.shift_right_logical(ids, 7)
    low = bits(iota((128, keep), 0) == lax.bitwise_and(ids, 127))
    per = mask_ref.shape[0] // 128
    count = blocks // 128 // per
    for t in range(per):
        hit = bits(iota((128, keep), 0) == high - t * count)
        mask_ref[t * 128 : (t + 1) * 128, :] = nt(low, hit)
    outbox[...] = jnp.zeros_like(outbox)
    for o in range(owners):
        outbox[o * ROWS + SLOTS : o * ROWS + SLOTS + 1, :] = tags[o : o + 1, :]

    def widen(i, carry):
        rows = pl.ds(pl.multiple_of(i * chunk, chunk), chunk)
        wide[rows, :] = held[rows, :].astype(F32)
        return carry

    for p, load in enumerate(loads):
        load.wait()
        lax.fori_loop(p * part // chunk, (p + 1) * part // chunk, widen, 0)
    fetch.wait()

    def move(k, carry):
        outbox[pl.ds(spot_s[0, k], 1), :] = wide[pl.ds(kept_ref[0, 0, k], 1), :]
        return carry

    lax.fori_loop(0, keep, move, 0, unroll=16)
    for o in range(owners):
        send_ref[o] = outbox[o * ROWS : (o + 1) * ROWS, :].astype(BF)
    for copy in packs:
        copy.wait()


def prep(me, my, kept, lengths, table, activ, key_grad, owners, tiles):
    tokens, keys = key_grad.shape
    blocks, width = table.shape
    keep = kept.shape[2]
    smem = pl.BlockSpec(memory_space=SMEM)
    vmem = pl.BlockSpec(memory_space=VMEM)
    whole = pl.BlockSpec(memory_space=pltpu.HBM)
    return pl.pallas_call(
        prep_kernel,
        out_shape=(
            jax.ShapeDtypeStruct((owners, ROWS, width), BF),
            jax.ShapeDtypeStruct((tiles * 128, 128), F32),
            jax.ShapeDtypeStruct((tokens, keys + activ.shape[1] // 4), BF),
        ),
        in_specs=[smem, smem, smem, vmem, vmem, whole, whole, whole],
        out_specs=(vmem, vmem, vmem),
        scratch_shapes=[
            VMEM((blocks, width), BF),
            VMEM((blocks, width), F32),
            VMEM((owners * ROWS, width), F32),
            VMEM((1, keep), jnp.int32),
            SMEM((1, keep), jnp.int32),
            pltpu.SemaphoreType.DMA((4,)),
            pltpu.SemaphoreType.DMA,
            pltpu.SemaphoreType.DMA((2,)),
        ],
        compiler_params=pltpu.CompilerParams(vmem_limit_bytes=PREP_LIMIT << 20),
        cost_estimate=pl.CostEstimate(flops=30_000_000, bytes_accessed=4 * blocks * width, transcendentals=0),
        name="prep",
    )(me, my, kept, kept, lengths, table, activ, key_grad)


def owned_kernel(got_ref, out_ref):
    region_max = out_ref.shape[0]
    row_id = lax.broadcasted_iota(jnp.int32, (region_max, 128), 0).astype(F32) + 1.0
    total = jnp.zeros(out_ref.shape, F32)
    for g in range(got_ref.shape[0] // GROUP):
        part = got_ref[g * GROUP : (g + 1) * GROUP]
        tags = jnp.sum(part[:, SLOTS, :].astype(F32), axis=0, keepdims=True)
        pick = (row_id == tags).astype(F32).astype(BF)
        rows = part[:, :SLOTS, :].reshape(GROUP * SLOTS, 128)
        total += jnp.dot(pick, rows, preferred_element_type=F32)
    out_ref[...] = total


def owned(got, region_max):
    return pl.pallas_call(
        owned_kernel,
        out_shape=jax.ShapeDtypeStruct((region_max, got.shape[2]), F32),
        in_specs=[pl.BlockSpec(memory_space=VMEM)],
        out_specs=pl.BlockSpec(memory_space=VMEM),
        compiler_params=pltpu.CompilerParams(vmem_limit_bytes=4 << 20),
        cost_estimate=pl.CostEstimate(flops=4_000_000, bytes_accessed=got.size * 2, transcendentals=0),
        name="owned",
    )(got)


def grad_kernel(my_ref, a0, g0, b1, b2, b3, g1, g3, feed_ref, mask_ref, out_ref, spread, grads):
    tile = a0.shape[1]
    tokens, keys = g0.shape
    per = keys // 128
    step = pl.program_id(0)
    near = pl.ds(pl.multiple_of(step * tile, 128), tile)
    column = pl.ds(pl.multiple_of(keys + step * tile, 128), tile)

    @pl.when(step == 0)
    def _():
        grads[:tokens, :] = g0[...]
        grads[tokens : 2 * tokens, :] = g1[...]
        grads[2 * tokens : 3 * tokens, :] = b2[:, :keys]
        grads[3 * tokens :, :] = g3[...]

    acts = jnp.concatenate([a0[...], b1[:, near], b2[:, column], b3[:, near]], axis=0)
    total = lax.dot_general(acts, grads[...], (((0,), (0,)), ((), ())), preferred_element_type=F32)
    for j in range(per):
        spread[pl.ds(j, tile, stride=per), :] = total[:, j * 128 : (j + 1) * 128]
    mask = mask_ref[...]
    for i in range(tile * per // 128):
        rows = slice(i * 128, (i + 1) * 128)
        feed = feed_ref[rows, :].astype(F32)
        out_ref[rows, :] = (jnp.where(mask[:, i : i + 1] > 0.0, 0.0, feed) + spread[rows, :]).astype(BF)


def grad_update(my, activ, key_grad, bundles, near, table, mask):
    tile = TILE
    tokens, keys = key_grad.shape
    features = bundles[0].shape[1]
    per = keys // 128
    steps = features // tile
    vmem = pl.BlockSpec(memory_space=VMEM)
    rows = pl.BlockSpec((tile * per, 128), lambda t, my: (t, 0))
    return pl.pallas_call(
        grad_kernel,
        out_shape=jax.ShapeDtypeStruct(table.shape, BF),
        grid_spec=pltpu.PrefetchScalarGridSpec(
            num_scalar_prefetch=1,
            grid=(steps,),
            in_specs=[pl.BlockSpec((tokens, tile), lambda t, my: (0, my[0] * steps + t))]
            + [vmem] * 6 + [rows, pl.BlockSpec((128, 128), lambda t, my: (t, 0))],
            out_specs=rows,
            scratch_shapes=[VMEM((tile * per, 128), F32), VMEM((4 * tokens, keys), BF)],
        ),
        compiler_params=pltpu.CompilerParams(vmem_limit_bytes=GRAD_LIMIT << 20),
        cost_estimate=pl.CostEstimate(
            flops=2 * 4 * tokens * features * keys, bytes_accessed=12 << 20, transcendentals=0
        ),
        name="grad_update",
    )(my, activ, key_grad, *bundles, *near, table, mask)


def join_kernel(*refs):
    out_ref = refs[-1]
    rows = refs[0].shape[0]
    for i, ref in enumerate(refs[:-1]):
        out_ref[i * rows : (i + 1) * rows, :] = ref[...]


def join(pieces):
    rows, width = pieces[0].shape
    total = len(pieces) * rows
    return pl.pallas_call(
        join_kernel,
        out_shape=jax.ShapeDtypeStruct((total, width), BF),
        in_specs=[pl.BlockSpec(memory_space=VMEM)] * len(pieces),
        out_specs=pl.BlockSpec(memory_space=VMEM),
        compiler_params=pltpu.CompilerParams(vmem_limit_bytes=8 << 20),
        cost_estimate=pl.CostEstimate(flops=500_000, bytes_accessed=4 * total * width, transcendentals=0),
        name="join",
    )(*pieces)


def dots_kernel(my_ref, g0, b1, b3, weight_ref, p0, p1, p3):
    tokens = g0.shape[0]
    grads = jnp.concatenate([g0[...], b1[...], b3[...]], axis=0)
    product = nt(grads, weight_ref[...]).astype(BF)
    for i, out in enumerate((p0, p1, p3)):
        out[...] = product[i * tokens : (i + 1) * tokens, :]


def dots(my, key_grad, near, weight):
    tokens, keys = key_grad.shape
    features = weight.shape[0]
    tile = DOTS_TILE
    steps = features // tile
    grads = pl.BlockSpec((tokens, keys), lambda t, my: (0, 0))
    out = pl.BlockSpec((tokens, tile), lambda t, my: (0, t))
    return pl.pallas_call(
        dots_kernel,
        out_shape=(jax.ShapeDtypeStruct((tokens, 4 * features), BF),)
        + (jax.ShapeDtypeStruct((tokens, features), BF),) * 2,
        grid_spec=pltpu.PrefetchScalarGridSpec(
            num_scalar_prefetch=1,
            grid=(steps,),
            in_specs=[grads, grads, grads, pl.BlockSpec((tile, keys), lambda t, my: (t, 0))],
            out_specs=(pl.BlockSpec((tokens, tile), lambda t, my: (0, my[0] * steps + t)), out, out),
        ),
        compiler_params=pltpu.CompilerParams(vmem_limit_bytes=DOTS_LIMIT << 20),
        cost_estimate=pl.CostEstimate(
            flops=2 * 3 * tokens * features * keys, bytes_accessed=5 << 20, transcendentals=0
        ),
        name="dots",
    )(my, key_grad, near[0], near[1], weight)


def finish_kernel(my_ref, where_ref, grad_ref, near_ref, other_ref, p1, p3, begun_ref, out_ref, far, sems):
    half, _ = near_ref.shape
    width = p1.shape[1]
    y, z, core = where_ref[0], where_ref[1], where_ref[2]
    piece = half // 8

    def column(j):
        return pl.multiple_of(lax.rem(my_ref[0] + 4 - j, 4) * width, width)

    copies = []
    for j, ref in ((1, p1), (3, p3)):
        copy = pltpu.make_async_copy(ref, out_ref.at[:, pl.ds(column(j), width)], sems.at[j])
        copy.start()
        copies.append(copy)

    def fetch(ref, row, residue):
        turn_y = lax.rem(row + 4 - y, 4)
        turn_z = lax.rem(residue + z, 2)
        return ref[pl.ds(pl.multiple_of((turn_y * 2 + turn_z) * piece, piece), piece), :]

    grads = grad_ref[...]
    for source in range(2):
        ref = near_ref if source == 0 else other_ref
        side = core if source == 0 else 1 - core
        for row in range(4):
            rows = jnp.concatenate([fetch(ref, row, residue) for residue in range(2)], axis=0)
            at = pl.multiple_of(side * half + row * 2 * piece, 2 * piece)
            far[:, pl.ds(at, 2 * piece)] = nt(grads, rows).astype(BF)
    copy = pltpu.make_async_copy(far, out_ref.at[:, pl.ds(column(2), width)], sems.at[2])
    copy.start()
    copies.append(copy)
    for copy in copies:
        copy.wait()


def finish(my, where, key_grad, near, other, p1, p3, begun):
    tokens, width = p1.shape
    vmem = pl.BlockSpec(memory_space=VMEM)
    smem = pl.BlockSpec(memory_space=SMEM)
    return pl.pallas_call(
        finish_kernel,
        out_shape=jax.ShapeDtypeStruct((tokens, 4 * width), BF),
        in_specs=[smem, smem] + [vmem] * 5 + [pl.BlockSpec(memory_space=pltpu.HBM)],
        out_specs=pl.BlockSpec(memory_space=pltpu.HBM),
        input_output_aliases={7: 0},
        scratch_shapes=[VMEM((tokens, width), BF), pltpu.SemaphoreType.DMA((4,))],
        compiler_params=pltpu.CompilerParams(vmem_limit_bytes=16 << 20),
        cost_estimate=pl.CostEstimate(flops=300_000_000, bytes_accessed=6 << 20, transcendentals=0),
        name="finish",
    )(my, where, key_grad, near, other, p1, p3, begun)


def shift(x, k, n=4):
    return lax.ppermute(x, "shard", [(i, (i + k) % n) for i in range(n)])


def after(x, *earlier):
    return lax.optimization_barrier((x, *earlier))[0]


def turn(x, dy, dz, dc):
    pairs = []
    for y in range(4):
        for z in range(8):
            for c in range(2):
                to = (((y + dy) % 4) * 8 + (z ^ dz)) * 2 + (c ^ dc)
                pairs.append(((y * 8 + z) * 2 + c, to))
    return lax.ppermute(x, "rep", pairs)


def step(activ, key_grad, key_weight, feedback, kept, region_len):
    shards = lax.axis_size("shard")
    my = lax.axis_index("shard")
    rep = lax.axis_index("rep")
    me = rep.reshape(1)
    my1 = my.reshape(1)
    y, z, core = lax.div(rep, 16), lax.rem(lax.div(rep, 2), 8), lax.rem(rep, 2)
    where = jnp.stack([y, z, core])
    owners = lax.axis_size("rep")
    width = activ.shape[1] // shards
    piece = width // 16
    index = ((core * 4 + y) * 2 + lax.rem(z, 2)).reshape(1)
    grad_one = shift(key_grad, 1)
    grad_three = shift(key_grad, 3)
    one, three, mine = pack(my1, index, activ, key_weight, width, piece)
    mine = shift(mine, 2)
    bundle, back = {}, {}
    bundle[1] = shift(one, 1)
    bundle[3] = shift(three, 3)
    twin = turn(mine, 0, 1, 0)
    table = feedback[0]
    blocks = table.shape[0]
    mean_len = blocks // owners
    send, mask, two = prep(me, my1, kept, region_len, table, activ, key_grad, owners, width // TILE)
    bundle[2] = shift(two, 2)
    plane = join([mine, twin])
    grid = [plane, None, None, None]
    for dy in (1, 3, 2):
        grid[dy] = turn(plane, -dy, 0, 0)
    got = lax.all_to_all(send, "rep", split_axis=0, concat_axis=0, tiled=True)
    begun, *parts = dots(my1, key_grad, [grad_one, grad_three], key_weight)
    for k, part in zip((1, 3), parts):
        back[k] = shift(part, shards - k)
    near = join(grid)
    other = turn(near, 0, 0, 1)
    updated = grad_update(my1, activ, key_grad, [bundle[1], bundle[2], bundle[3]], [grad_one, grad_three], table, mask)
    owned_rows = owned(got, mean_len + mean_len // 2)
    last = after(back[1], owned_rows, updated)
    input_grad = finish(my1, where, key_grad, near, other, back[3], last, begun)
    return (input_grad, updated[None], owned_rows[None])


def solution(mesh):
    return jax.shard_map(
        step,
        mesh=mesh,
        in_specs=(
            P(("rep", "shard"), None),
            P(("rep", "shard"), None),
            P("shard", None),
            P("rep", "shard", None),
            P("rep", "shard", None),
            P("shard", None),
        ),
        out_specs=(P(("rep", "shard"), None), P("rep", "shard", None), P("shard", "rep", None)),
        check_vma=False,
    )
```

time: 74.2 us -> 92.9 us (1.25)
  waiting for transfers between devices: 13.2 us -> 36.5 us
  matrix products: 8.94 us -> 0 us
  starting transfers between devices: 26.8 us -> 32.3 us
  Pallas kernels: 23.1 us -> 20.7 us
    ppermute x0 -> x5, waiting for transfers between devices: none -> 15.2 us  [turn(): return lax.ppermute(x, 'rep', pairs)]
    dot_general x4 -> x0, matrix products: 8.94 us -> none  [nt_dot(): lax.dot_general(a, b, (((1,), (1,)), ((), ())), preferred_element_type=F32)]
    ppermute x9 -> x8, waiting for transfers between devices: 13.2 us -> 21.3 us  [shift(): return lax.ppermute(x, 'shard', [(i, (i + k) % n) for i in range(n)])]
    ppermute x0 -> x5, starting transfers between devices: none -> 7.01 us  [turn(): return lax.ppermute(x, 'rep', pairs)]
    pallas_call x1, Pallas kernels: 8.7 us -> 4.46 us  [prep(): pl.pallas_call(prep_kernel, out_shape=(jax.ShapeDtypeStruct((owners, ROWS...]
    pallas_call x3 -> x6, Pallas kernels: 13.3 us -> 15.2 us  [the longest x1 5.88 us: grad_update(): pl.pallas_call(grad_kernel, out_shape=jax.ShapeDtypeStruct(table.shape, B...]
    ppermute x9 -> x8, starting transfers between devices: 14.7 us -> 13.7 us  [shift(): return lax.ppermute(x, 'shard', [(i, (i + k) % n) for i in range(n)])]
  transfers between devices with their start and end apart: 10 -> 14, of which waited for: 3 -> 8; matrix products, arithmetic and copies ran while one was open for 12% -> 0% of each run, Pallas kernels for 28% -> 16%
where the time goes in v3:
time: 92.9 us; the launch traced here: 92.2 us
  waiting for transfers between devices  36.5 us (39%)
  starting transfers between devices  32.3 us (35%)
  Pallas kernels  20.7 us (22%)
  local copies, waits for them, and re-layouts  1.74 us (2%)
    ppermute x8, waiting for transfers between devices, shift(): return lax.ppermute(x, 'shard', [(i, (i + k) % n) for i in range(n)])  21.3 us
    ppermute x5, waiting for transfers between devices, turn(): return lax.ppermute(x, 'rep', pairs)  15.2 us
    ppermute x8, starting transfers between devices, shift(): return lax.ppermute(x, 'shard', [(i, (i + k) % n) for i in range(n)])  13.7 us
    all_to_all x1, starting transfers between devices, step(): got = lax.all_to_all(send, 'rep', split_axis=0, concat_axis=0, tiled=True)  11.7 us
    ppermute x5, starting transfers between devices, turn(): return lax.ppermute(x, 'rep', pairs)  7.01 us
    pallas_call x1, Pallas kernels, grad_update(): pl.pallas_call(grad_kernel, out_shape=jax.ShapeDtypeStruct(table.shape, B...  5.88 us
    pallas_call x1, Pallas kernels, prep(): pl.pallas_call(prep_kernel, out_shape=(jax.ShapeDtypeStruct((owners, ROWS...  4.46 us
    pallas_call x1, Pallas kernels, dots(): pl.pallas_call(dots_kernel, out_shape=(jax.ShapeDtypeStruct((tokens, 4 *...  3.59 us
  transfers between devices with their start and end apart: 14, of which 8 were waited for; matrix products, arithmetic and copies ran while one was open for 0% of the time, Pallas kernels for 16%

profile of v3, /device:TPU:8, one launch (start us, length us, event | category | flops | bytes accessed | tf_op | source)
XLA Modules:
  0.0 92.2 jit_solution(10251234494526061257)
XLA Ops:
  0.7 2.3 %pack.1 = (bf16[128,2048]{1,0:T(8,128)(2,1)}, bf16[128,2048]{1,0:T(8,128)(2,1)}, bf16[128,640]{1,0:T(8,128)(2,1)}) custom-call(s32[1]{0:T(128)} %bitcast.my_ref, s32[1]{0:T(128)} %bitcast.4.index_ref, bf16[128,8192]{1,0:T(8,128)(2,1)} %a0.1, bf16[2048,640]{1,0:T(8,128)(2,1)} %weight_ref.3), custom_call_target="tpu_custom_call" | custom-call | flops 1000000 | bytes 3145728 | tf_op jit(solution)/shard_map/pack/pallas_call | solution.py:52
  3.0 3.1 %collective-permute-start = (bf16[128,640]{1,0:T(8,128)(2,1)}, bf16[128,640]{1,0:T(8,128)(2,1)S(1)}, u32[]{:S(2)}, u32[]{:S(2)}) collective-permute-start(bf16[128,640]{1,0:T(8,128)(2,1)} %get-tuple-element.13), channel_id=1, source_target_pairs={{0,2},{1,3},{2,0},{3,1},{4,6},{5,7},{6,4},{7,5},{8,10},{9,11},{10,... | collective-permute-start | bytes 491528 | tf_op jit(solution)/shard_map/ppermute | solution.py:366
  6.1 4.6 %collective-permute-done.refs_0_ = bf16[128,640]{1,0:T(8,128)(2,1)S(1)} collective-permute-done((bf16[128,640]{1,0:T(8,128)(2,1)}, bf16[128,640]{1,0:T(8,128)(2,1)S(1)}, u32[]{:S(2)}, u32[]{:S(2)}) %collective-permute-start) | collective-permute-done | bytes 163872 | tf_op jit(solution)/shard_map/ppermute | solution.py:366
  10.7 1.9 %collective-permute-start.1 = (bf16[128,640]{1,0:T(8,128)(2,1)S(1)}, bf16[128,640]{1,0:T(8,128)(2,1)S(1)}, u32[]{:S(2)}, u32[]{:S(2)}) collective-permute-start(bf16[128,640]{1,0:T(8,128)(2,1)S(1)} %collective-permute-done.refs_0_), channel_id=1, source_target_pairs={{0,8},{4,12},{8,0},{12,4},{16,24},{20,28},{24,16},{28,20},{32,40},... | collective-permute-start | bytes 491528 | tf_op jit(solution)/shard_map/ppermute | solution.py:380
  12.7 3.4 %collective-permute-done.1.refs_1_ = bf16[128,640]{1,0:T(8,128)(2,1)S(1)} collective-permute-done((bf16[128,640]{1,0:T(8,128)(2,1)S(1)}, bf16[128,640]{1,0:T(8,128)(2,1)S(1)}, u32[]{:S(2)}, u32[]{:S(2)}) %collective-permute-start.1) | collective-permute-done | bytes 163872 | tf_op jit(solution)/shard_map/ppermute | solution.py:380
  16.1 1.7 %collective-permute-start.4 = (bf16[256,640]{1,0:T(8,128)(2,1)S(1)}, bf16[256,640]{1,0:T(8,128)(2,1)S(1)}, u32[]{:S(2)}, u32[]{:S(2)}) collective-permute-start(bf16[256,640]{1,0:T(8,128)(2,1)S(1)} %join.2.refs_0_), channel_id=1, source_target_pairs={{0,64},{4,68},{8,72},{12,76},{16,80},{20,84},{24,88},{28,92},{32,9... | collective-permute-start | bytes 983048 | tf_op jit(solution)/shard_map/ppermute | solution.py:380
  17.7 2.0 %collective-permute-start.3 = (bf16[256,640]{1,0:T(8,128)(2,1)S(1)}, bf16[256,640]{1,0:T(8,128)(2,1)S(1)}, u32[]{:S(2)}, u32[]{:S(2)}) collective-permute-start(bf16[256,640]{1,0:T(8,128)(2,1)S(1)} %join.2.refs_0_), channel_id=1, source_target_pairs={{0,128},{4,132},{8,136},{12,140},{16,144},{20,148},{24,152},{28,15... | collective-permute-start | bytes 983048 | tf_op jit(solution)/shard_map/ppermute | solution.py:380
  19.8 1.3 %collective-permute-start.2 = (bf16[256,640]{1,0:T(8,128)(2,1)S(1)}, bf16[256,640]{1,0:T(8,128)(2,1)S(1)}, u32[]{:S(2)}, u32[]{:S(2)}) collective-permute-start(bf16[256,640]{1,0:T(8,128)(2,1)S(1)} %join.2.refs_0_), channel_id=1, source_target_pairs={{0,192},{4,196},{8,200},{12,204},{16,208},{20,212},{24,216},{28,22... | collective-permute-start | bytes 983048 | tf_op jit(solution)/shard_map/ppermute | solution.py:380
  21.1 5.7 %collective-permute-done.4.refs_3_ = bf16[256,640]{1,0:T(8,128)(2,1)S(1)} collective-permute-done((bf16[256,640]{1,0:T(8,128)(2,1)S(1)}, bf16[256,640]{1,0:T(8,128)(2,1)S(1)}, u32[]{:S(2)}, u32[]{:S(2)}) %collective-permute-start.4) | collective-permute-done | bytes 327712 | tf_op jit(solution)/shard_map/ppermute | solution.py:380
  26.7 3.1 %collective-permute-done.3.refs_2_ = bf16[256,640]{1,0:T(8,128)(2,1)S(1)} collective-permute-done((bf16[256,640]{1,0:T(8,128)(2,1)S(1)}, bf16[256,640]{1,0:T(8,128)(2,1)S(1)}, u32[]{:S(2)}, u32[]{:S(2)}) %collective-permute-start.3) | collective-permute-done | bytes 327712 | tf_op jit(solution)/shard_map/ppermute | solution.py:380
  29.8 3.1 %collective-permute-done.2.refs_1_ = bf16[256,640]{1,0:T(8,128)(2,1)S(1)} collective-permute-done((bf16[256,640]{1,0:T(8,128)(2,1)S(1)}, bf16[256,640]{1,0:T(8,128)(2,1)S(1)}, u32[]{:S(2)}, u32[]{:S(2)}) %collective-permute-start.2) | collective-permute-done | bytes 327712 | tf_op jit(solution)/shard_map/ppermute | solution.py:380
  32.9 0.1 join.3.near_ref
  33.0 0.1 collective-permute-start.5
  33.1 1.6 %collective-permute-start.10 = (bf16[128,2048]{1,0:T(8,128)(2,1)}, bf16[128,2048]{1,0:T(8,128)(2,1)S(1)}, u32[]{:S(2)}, u32[]{:S(2)}) collective-permute-start(bf16[128,2048]{1,0:T(8,128)(2,1)} %get-tuple-element.17), channel_id=1, source_target_pairs={{0,1},{1,2},{2,3},{3,0},{4,5},{5,6},{6,7},{7,4},{8,9},{9,10},{10,1... | collective-permute-start | bytes 1572872 | tf_op jit(solution)/shard_map/ppermute | solution.py:366
  34.7 1.7 %collective-permute-start.7 = (bf16[128,640]{1,0:T(8,128)(2,1)}, bf16[128,640]{1,0:T(8,128)(2,1)}, u32[]{:S(2)}, u32[]{:S(2)}) collective-permute-start(bf16[128,640]{1,0:T(8,128)(2,1)} %grad_ref.3), channel_id=1, source_target_pairs={{0,3},{1,0},{2,1},{3,2},{4,7},{5,4},{6,5},{7,6},{8,11},{9,8},{10,9... | collective-permute-start | bytes 491528 | tf_op jit(solution)/shard_map/ppermute | solution.py:366
  36.4 4.5 %prep.1 = (bf16[64,24,128]{2,1,0:T(8,128)(2,1)}, f32[256,128]{1,0:T(8,128)}, bf16[128,2688]{1,0:T(8,128)(2,1)}) custom-call(s32[1]{0:T(128)} %bitcast.5.me_ref, s32[1]{0:T(128)} %bitcast.my_ref, s32[1,1,512]{2,1,0:T(1,128)} %ids_ref.1, s32[1,1,512]{2,1,0:T(1,128)} %ids_ref.1, s32[1,64]{1,0:T(1,128)} %len_ref.1, bf16[10240,128]{1,0:T(8,128)(2,1)} %bitcast.9, ...), custom_call_target="tpu_custom_call" | custom-call | flops 30000000 | bytes 5242880 | tf_op jit(solution)/shard_map/prep/pallas_call | solution.py:156
  40.9 1.9 %collective-permute-start.11 = (bf16[128,2688]{1,0:T(8,128)(2,1)}, bf16[128,2688]{1,0:T(8,128)(2,1)}, u32[]{:S(2)}, u32[]{:S(2)}) collective-permute-start(bf16[128,2688]{1,0:T(8,128)(2,1)} %get-tuple-element.18), channel_id=1, source_target_pairs={{0,2},{1,3},{2,0},{3,1},{4,6},{5,7},{6,4},{7,5},{8,10},{9,11},{10,... | collective-permute-start | bytes 2064392 | tf_op jit(solution)/shard_map/ppermute | solution.py:366
  42.8 0.6 collective-permute-start.6
  43.4 11.7 %all-to-all-start = ((bf16[64,24,128]{2,1,0:T(8,128)(2,1)}), bf16[64,24,128]{2,1,0:T(8,128)(2,1)S(1)}, u32[]{:S(2)}, u32[]{:S(2)}) async-start(bf16[64,24,128]{2,1,0:T(8,128)(2,1)} %get-tuple-element.16), calls=%async_computation | async-start | bytes 786432 | tf_op jit(solution)/shard_map/all_to_all | solution.py:412
  55.1 0.0 collective-permute-done.7.b3.g3
  55.1 2.7 %collective-permute-start.12 = (bf16[128,2048]{1,0:T(8,128)(2,1)}, bf16[128,2048]{1,0:T(8,128)(2,1)S(1)}, u32[]{:S(2)}, u32[]{:S(2)}) collective-permute-start(bf16[128,2048]{1,0:T(8,128)(2,1)} %get-tuple-element.19), channel_id=1, source_target_pairs={{0,3},{1,0},{2,1},{3,2},{4,7},{5,4},{6,5},{7,6},{8,11},{9,8},{10,9... | collective-permute-start | bytes 1572872 | tf_op jit(solution)/shard_map/ppermute | solution.py:366
  57.8 9.5 %collective-permute-done.6.b1.g1 = bf16[128,640]{1,0:T(8,128)(2,1)} collective-permute-done((bf16[128,640]{1,0:T(8,128)(2,1)}, bf16[128,640]{1,0:T(8,128)(2,1)}, u32[]{:S(2)}, u32[]{:S(2)}) %collective-permute-start.6) | collective-permute-done | bytes 163872 | tf_op jit(solution)/shard_map/ppermute | solution.py:366
  67.2 0.0 copy-start
  67.2 1.7 %copy-done = bf16[2048,640]{1,0:T(8,128)(2,1)S(1)} copy-done((bf16[2048,640]{1,0:T(8,128)(2,1)S(1)}, bf16[2048,640]{1,0:T(8,128)(2,1)}, u32[]{:S(2)}) %copy-start) | copy-done | bytes 2621464
  69.0 0.0 copy-start.1
  69.0 3.6 %dots.1 = (bf16[128,8192]{1,0:T(8,128)(2,1)}, bf16[128,2048]{1,0:T(8,128)(2,1)}, bf16[128,2048]{1,0:T(8,128)(2,1)}) custom-call(s32[1]{0:T(128)} %bitcast.my_ref, bf16[128,640]{1,0:T(8,128)(2,1)} %grad_ref.3, bf16[128,640]{1,0:T(8,128)(2,1)} %collective-permute-done.6.b1.g1, bf16[128,640]{1,0:T(8,128)(2,1)} %collective-permute-done.7.b3.g3, ...), custom_call_target="tpu_custom_call" | custom-call | flops 1006632960 | bytes 5242880 | tf_op jit(solution)/shard_map/dots/pallas_call | solution.py:295
  72.6 1.6 %collective-permute-start.9 = (bf16[128,2048]{1,0:T(8,128)(2,1)}, bf16[128,2048]{1,0:T(8,128)(2,1)}, u32[]{:S(2)}, u32[]{:S(2)}) collective-permute-start(bf16[128,2048]{1,0:T(8,128)(2,1)} %get-tuple-element.15), channel_id=1, source_target_pairs={{0,3},{1,0},{2,1},{3,2},{4,7},{5,4},{6,5},{7,6},{8,11},{9,8},{10,9... | collective-permute-start | bytes 1572872 | tf_op jit(solution)/shard_map/ppermute | solution.py:366
  74.2 0.0 collective-permute-done.10.b1
  74.2 0.4 collective-permute-start.8
  74.6 0.1 pad_add_fusion.where_ref
  74.7 0.0 collective-permute-done.12.b3
  74.7 0.0 collective-permute-done.11.b2
  74.7 0.0 copy-done.1
  74.7 5.9 %grad_update.1 = bf16[10240,128]{1,0:T(8,128)(2,1)} custom-call(s32[1]{0:T(128)} %bitcast.my_ref, bf16[128,8192]{1,0:T(8,128)(2,1)} %a0.1, bf16[128,640]{1,0:T(8,128)(2,1)} %grad_ref.3, bf16[128,2048]{1,0:T(8,128)(2,1)S(1)} %collective-permute-done.10.b1, bf16[128,2688]{1,0:T(8,128)(2,1)} %collective-permute-done.11.b2, ...), custom_call_target="tpu_custom_call" | custom-call | flops 1342177280 | bytes 12582912 | tf_op jit(solution)/shard_map/grad_update/pallas_call | solution.py:240
  80.6 0.0 all-to-all-done.got_ref
  80.6 1.1 %owned.1 = f32[240,128]{1,0:T(8,128)} custom-call(bf16[64,24,128]{2,1,0:T(8,128)(2,1)S(1)} %all-to-all-done.got_ref), custom_call_target="tpu_custom_call" | custom-call | flops 4000000 | bytes 393216 | tf_op jit(solution)/shard_map/owned/pallas_call | solution.py:195
  81.6 4.7 %collective-permute-done.9.p3 = bf16[128,2048]{1,0:T(8,128)(2,1)} collective-permute-done((bf16[128,2048]{1,0:T(8,128)(2,1)}, bf16[128,2048]{1,0:T(8,128)(2,1)}, u32[]{:S(2)}, u32[]{:S(2)}) %collective-permute-start.9) | collective-permute-done | bytes 524320 | tf_op jit(solution)/shard_map/ppermute | solution.py:366
  86.3 2.5 %collective-permute-done.8.p1 = bf16[128,2048]{1,0:T(8,128)(2,1)} collective-permute-done((bf16[128,2048]{1,0:T(8,128)(2,1)}, bf16[128,2048]{1,0:T(8,128)(2,1)}, u32[]{:S(2)}, u32[]{:S(2)}) %collective-permute-start.8) | collective-permute-done | bytes 524320 | tf_op jit(solution)/shard_map/ppermute | solution.py:366
  88.8 0.0 collective-permute-done.5.other_ref
  88.8 3.3 %finish.1 = bf16[128,8192]{1,0:T(8,128)(2,1)} custom-call(s32[1]{0:T(128)} %bitcast.my_ref, s32[3]{0:T(128)S(1)} %pad_add_fusion.where_ref, bf16[128,640]{1,0:T(8,128)(2,1)} %grad_ref.3, bf16[1024,640]{1,0:T(8,128)(2,1)S(1)} %join.3.near_ref, bf16[1024,640]{1,0:T(8,128)(2,1)S(1)} %collective-permute-done.5.other_ref, ...), custom_call_target="tpu_custom_call", output_to_operand_aliasing={{}: (7, {})} | custom-call | flops 300000000 | bytes 6291456 | tf_op jit(solution)/shard_map/finish/pallas_call | solution.py:352
  (1 shorter events, 0.0 us)
Async XLA Ops:
  3.0 7.7 %collective-permute-start = (bf16[128,640]{1,0:T(8,128)(2,1)}, bf16[128,640]{1,0:T(8,128)(2,1)S(1)}, u32[]{:S(2)}, u32[]{:S(2)}) collective-permute-start(bf16[128,640]{1,0:T(8,128)(2,1)} %get-tuple-element.13), channel_id=1, source_target_pairs={{0,2},{1,3},{2,0},{3,1},{4,6},{5,7},{6,4},{7,5},{8,10},{9,11},{10,... | collective-permute-start | bytes 491528 | tf_op jit(solution)/shard_map/ppermute | solution.py:366
  10.7 5.3 %collective-permute-start.1 = (bf16[128,640]{1,0:T(8,128)(2,1)S(1)}, bf16[128,640]{1,0:T(8,128)(2,1)S(1)}, u32[]{:S(2)}, u32[]{:S(2)}) collective-permute-start(bf16[128,640]{1,0:T(8,128)(2,1)S(1)} %collective-permute-done.refs_0_), channel_id=1, source_target_pairs={{0,8},{4,12},{8,0},{12,4},{16,24},{20,28},{24,16},{28,20},{32,40},... | collective-permute-start | bytes 491528 | tf_op jit(solution)/shard_map/ppermute | solution.py:380
  16.1 10.7 %collective-permute-start.4 = (bf16[256,640]{1,0:T(8,128)(2,1)S(1)}, bf16[256,640]{1,0:T(8,128)(2,1)S(1)}, u32[]{:S(2)}, u32[]{:S(2)}) collective-permute-start(bf16[256,640]{1,0:T(8,128)(2,1)S(1)} %join.2.refs_0_), channel_id=1, source_target_pairs={{0,64},{4,68},{8,72},{12,76},{16,80},{20,84},{24,88},{28,92},{32,9... | collective-permute-start | bytes 983048 | tf_op jit(solution)/shard_map/ppermute | solution.py:380
  17.7 12.1 %collective-permute-start.3 = (bf16[256,640]{1,0:T(8,128)(2,1)S(1)}, bf16[256,640]{1,0:T(8,128)(2,1)S(1)}, u32[]{:S(2)}, u32[]{:S(2)}) collective-permute-start(bf16[256,640]{1,0:T(8,128)(2,1)S(1)} %join.2.refs_0_), channel_id=1, source_target_pairs={{0,128},{4,132},{8,136},{12,140},{16,144},{20,148},{24,152},{28,15... | collective-permute-start | bytes 983048 | tf_op jit(solution)/shard_map/ppermute | solution.py:380
  19.8 13.2 %collective-permute-start.2 = (bf16[256,640]{1,0:T(8,128)(2,1)S(1)}, bf16[256,640]{1,0:T(8,128)(2,1)S(1)}, u32[]{:S(2)}, u32[]{:S(2)}) collective-permute-start(bf16[256,640]{1,0:T(8,128)(2,1)S(1)} %join.2.refs_0_), channel_id=1, source_target_pairs={{0,192},{4,196},{8,200},{12,204},{16,208},{20,212},{24,216},{28,22... | collective-permute-start | bytes 983048 | tf_op jit(solution)/shard_map/ppermute | solution.py:380
  33.0 55.8 %collective-permute-start.5 = (bf16[1024,640]{1,0:T(8,128)(2,1)S(1)}, bf16[1024,640]{1,0:T(8,128)(2,1)S(1)}, u32[]{:S(2)}, u32[]{:S(2)}) collective-permute-start(bf16[1024,640]{1,0:T(8,128)(2,1)S(1)} %join.3.near_ref), channel_id=1, source_target_pairs={{0,4},{4,0},{8,12},{12,8},{16,20},{20,16},{24,28},{28,24},{32,36},... | collective-permute-start | bytes 3932168 | tf_op jit(solution)/shard_map/ppermute | solution.py:380
  33.1 41.0 %collective-permute-start.10 = (bf16[128,2048]{1,0:T(8,128)(2,1)}, bf16[128,2048]{1,0:T(8,128)(2,1)S(1)}, u32[]{:S(2)}, u32[]{:S(2)}) collective-permute-start(bf16[128,2048]{1,0:T(8,128)(2,1)} %get-tuple-element.17), channel_id=1, source_target_pairs={{0,1},{1,2},{2,3},{3,0},{4,5},{5,6},{6,7},{7,4},{8,9},{9,10},{10,1... | collective-permute-start | bytes 1572872 | tf_op jit(solution)/shard_map/ppermute | solution.py:366
  34.7 20.4 %collective-permute-start.7 = (bf16[128,640]{1,0:T(8,128)(2,1)}, bf16[128,640]{1,0:T(8,128)(2,1)}, u32[]{:S(2)}, u32[]{:S(2)}) collective-permute-start(bf16[128,640]{1,0:T(8,128)(2,1)} %grad_ref.3), channel_id=1, source_target_pairs={{0,3},{1,0},{2,1},{3,2},{4,7},{5,4},{6,5},{7,6},{8,11},{9,8},{10,9... | collective-permute-start | bytes 491528 | tf_op jit(solution)/shard_map/ppermute | solution.py:366
  40.9 33.8 %collective-permute-start.11 = (bf16[128,2688]{1,0:T(8,128)(2,1)}, bf16[128,2688]{1,0:T(8,128)(2,1)}, u32[]{:S(2)}, u32[]{:S(2)}) collective-permute-start(bf16[128,2688]{1,0:T(8,128)(2,1)} %get-tuple-element.18), channel_id=1, source_target_pairs={{0,2},{1,3},{2,0},{3,1},{4,6},{5,7},{6,4},{7,5},{8,10},{9,11},{10,... | collective-permute-start | bytes 2064392 | tf_op jit(solution)/shard_map/ppermute | solution.py:366
  42.8 24.4 %collective-permute-start.6 = (bf16[128,640]{1,0:T(8,128)(2,1)}, bf16[128,640]{1,0:T(8,128)(2,1)}, u32[]{:S(2)}, u32[]{:S(2)}) collective-permute-start(bf16[128,640]{1,0:T(8,128)(2,1)} %grad_ref.3), channel_id=1, source_target_pairs={{0,1},{1,2},{2,3},{3,0},{4,5},{5,6},{6,7},{7,4},{8,9},{9,10},{10,1... | collective-permute-start | bytes 491528 | tf_op jit(solution)/shard_map/ppermute | solution.py:366
  43.4 37.2 %all-to-all-start = ((bf16[64,24,128]{2,1,0:T(8,128)(2,1)}), bf16[64,24,128]{2,1,0:T(8,128)(2,1)S(1)}, u32[]{:S(2)}, u32[]{:S(2)}) async-start(bf16[64,24,128]{2,1,0:T(8,128)(2,1)} %get-tuple-element.16), calls=%async_computation | async-start | bytes 786432 | tf_op jit(solution)/shard_map/all_to_all | solution.py:412
  55.1 19.6 %collective-permute-start.12 = (bf16[128,2048]{1,0:T(8,128)(2,1)}, bf16[128,2048]{1,0:T(8,128)(2,1)S(1)}, u32[]{:S(2)}, u32[]{:S(2)}) collective-permute-start(bf16[128,2048]{1,0:T(8,128)(2,1)} %get-tuple-element.19), channel_id=1, source_target_pairs={{0,3},{1,0},{2,1},{3,2},{4,7},{5,4},{6,5},{7,6},{8,11},{9,8},{10,9... | collective-permute-start | bytes 1572872 | tf_op jit(solution)/shard_map/ppermute | solution.py:366
  67.2 1.7 %copy-start = (bf16[2048,640]{1,0:T(8,128)(2,1)S(1)}, bf16[2048,640]{1,0:T(8,128)(2,1)}, u32[]{:S(2)}) copy-start(bf16[2048,640]{1,0:T(8,128)(2,1)} %weight_ref.3) | copy-start | bytes 7864324
  69.0 5.7 %copy-start.1 = (f32[256,128]{1,0:T(8,128)S(1)}, f32[256,128]{1,0:T(8,128)}, u32[]{:S(2)}) copy-start(f32[256,128]{1,0:T(8,128)} %get-tuple-element.20.mask_ref) | copy-start | bytes 393220
  72.6 13.7 %collective-permute-start.9 = (bf16[128,2048]{1,0:T(8,128)(2,1)}, bf16[128,2048]{1,0:T(8,128)(2,1)}, u32[]{:S(2)}, u32[]{:S(2)}) collective-permute-start(bf16[128,2048]{1,0:T(8,128)(2,1)} %get-tuple-element.15), channel_id=1, source_target_pairs={{0,3},{1,0},{2,1},{3,2},{4,7},{5,4},{6,5},{7,6},{8,11},{9,8},{10,9... | collective-permute-start | bytes 1572872 | tf_op jit(solution)/shard_map/ppermute | solution.py:366
  74.2 14.6 %collective-permute-start.8 = (bf16[128,2048]{1,0:T(8,128)(2,1)}, bf16[128,2048]{1,0:T(8,128)(2,1)}, u32[]{:S(2)}, u32[]{:S(2)}) collective-permute-start(bf16[128,2048]{1,0:T(8,128)(2,1)} %get-tuple-element.14), channel_id=1, source_target_pairs={{0,1},{1,2},{2,3},{3,0},{4,5},{5,6},{6,7},{7,4},{8,9},{9,10},{10,1... | collective-permute-start | bytes 1572872 | tf_op jit(solution)/shard_map/ppermute | solution.py:366

commit v4 on v3

--- a/solution.py
+++ b/solution.py
@@ -16,9 +16,10 @@
 TILE = 1024
 PACK_LIMIT = 59
 PREP_LIMIT = 58
-GRAD_LIMIT = 50
+GRAD_LIMIT = 53
 DOTS_LIMIT = 40
 DOTS_TILE = 1024
+FINISH_LIMIT = 50
 
 
 def bundle_copies(my, k, activ_ref, grad_ref, out, sems):
@@ -75,7 +76,7 @@
 
 def prep_kernel(
     me_ref, my_ref, kept_ref, ids_ref, len_ref, table_ref, activ_ref, grad_ref,
-    send_ref, mask_ref, o2, held, wide, outbox, spot_v, spot_s, sems, spot_sem, pack_sems
+    send_ref, o2, held, wide, outbox, spot_v, spot_s, sems, spot_sem, pack_sems
 ):
     blocks = held.shape[0]
     owners = send_ref.shape[0]
@@ -114,13 +115,6 @@
     lane_base = lax.rem(me_ref[0], GROUP) * SLOTS
     lane = bits(iota((128, keep), 0) == slot.astype(jnp.int32) + lane_base)
     tags = nt((inside * (offset + 1.0)).astype(BF), lane)
-    high = lax.shift_right_logical(ids, 7)
-    low = bits(iota((128, keep), 0) == lax.bitwise_and(ids, 127))
-    per = mask_ref.shape[0] // 128
-    count = blocks // 128 // per
-    for t in range(per):
-        hit = bits(iota((128, keep), 0) == high - t * count)
-        mask_ref[t * 128 : (t + 1) * 128, :] = nt(low, hit)
     outbox[...] = jnp.zeros_like(outbox)
     for o in range(owners):
         outbox[o * ROWS + SLOTS : o * ROWS + SLOTS + 1, :] = tags[o : o + 1, :]
@@ -146,7 +140,7 @@
         copy.wait()
 
 
-def prep(me, my, kept, lengths, table, activ, key_grad, owners, tiles):
+def prep(me, my, kept, lengths, table, activ, key_grad, owners):
     tokens, keys = key_grad.shape
     blocks, width = table.shape
     keep = kept.shape[2]
@@ -157,11 +151,10 @@
         prep_kernel,
         out_shape=(
             jax.ShapeDtypeStruct((owners, ROWS, width), BF),
-            jax.ShapeDtypeStruct((tiles * 128, 128), F32),
             jax.ShapeDtypeStruct((tokens, keys + activ.shape[1] // 4), BF),
         ),
         in_specs=[smem, smem, smem, vmem, vmem, whole, whole, whole],
-        out_specs=(vmem, vmem, vmem),
+        out_specs=(vmem, vmem),
         scratch_shapes=[
             VMEM((blocks, width), BF),
             VMEM((blocks, width), F32),
@@ -203,7 +196,7 @@
     )(got)
 
 
-def grad_kernel(my_ref, a0, g0, b1, b2, b3, g1, g3, feed_ref, mask_ref, out_ref, spread, grads):
+def grad_kernel(my_ref, a0, g0, b1, b2, b3, g1, g3, feed_ref, ids_ref, out_ref, spread, grads):
     tile = a0.shape[1]
     tokens, keys = g0.shape
     per = keys // 128
@@ -222,14 +215,19 @@
     total = lax.dot_general(acts, grads[...], (((0,), (0,)), ((), ())), preferred_element_type=F32)
     for j in range(per):
         spread[pl.ds(j, tile, stride=per), :] = total[:, j * 128 : (j + 1) * 128]
-    mask = mask_ref[...]
+    ids = ids_ref[0]
+    keep = ids.shape[1]
+    count = tile * per // 128
+    low = bits(iota((128, keep), 0) == lax.bitwise_and(ids, 127))
+    hit = bits(iota((128, keep), 0) == lax.shift_right_logical(ids, 7) - step * count)
+    mask = nt(low, hit)
     for i in range(tile * per // 128):
         rows = slice(i * 128, (i + 1) * 128)
         feed = feed_ref[rows, :].astype(F32)
         out_ref[rows, :] = (jnp.where(mask[:, i : i + 1] > 0.0, 0.0, feed) + spread[rows, :]).astype(BF)
 
 
-def grad_update(my, activ, key_grad, bundles, near, table, mask):
+def grad_update(my, activ, key_grad, bundles, near, table, kept):
     tile = TILE
     tokens, keys = key_grad.shape
     features = bundles[0].shape[1]
@@ -244,16 +242,19 @@
             num_scalar_prefetch=1,
             grid=(steps,),
             in_specs=[pl.BlockSpec((tokens, tile), lambda t, my: (0, my[0] * steps + t))]
-            + [vmem] * 6 + [rows, pl.BlockSpec((128, 128), lambda t, my: (t, 0))],
+            + [vmem] * 6 + [rows, vmem],
             out_specs=rows,
-            scratch_shapes=[VMEM((tile * per, 128), F32), VMEM((4 * tokens, keys), BF)],
+            scratch_shapes=[
+                VMEM((tile * per, 128), F32),
+                VMEM((4 * tokens, keys), BF),
+            ],
         ),
         compiler_params=pltpu.CompilerParams(vmem_limit_bytes=GRAD_LIMIT << 20),
         cost_estimate=pl.CostEstimate(
             flops=2 * 4 * tokens * features * keys, bytes_accessed=12 << 20, transcendentals=0
         ),
         name="grad_update",
-    )(my, activ, key_grad, *bundles, *near, table, mask)
+    )(my, activ, key_grad, *bundles, *near, table, kept)
 
 
 def join_kernel(*refs):
@@ -310,54 +311,95 @@
     )(my, key_grad, near[0], near[1], weight)
 
 
-def finish_kernel(my_ref, where_ref, grad_ref, near_ref, other_ref, p1, p3, begun_ref, out_ref, far, sems):
-    half, _ = near_ref.shape
+def half_product(where_ref, grads, weight_ref, put):
+    half = weight_ref.shape[0]
+    y, z = where_ref[0], where_ref[1]
+    piece = half // 8
+    for row in range(4):
+        rows = []
+        for residue in range(2):
+            at = lax.rem(row + 4 - y, 4) * 2 + lax.rem(residue + z, 2)
+            rows.append(weight_ref[pl.ds(pl.multiple_of(at * piece, piece), piece), :])
+        put(row * 2 * piece, nt(grads, jnp.concatenate(rows, axis=0)).astype(BF))
+
+
+def far_kernel(where_ref, grad_ref, weight_ref, out_ref):
+    def put(column, value):
+        out_ref[:, column : column + value.shape[1]] = value
+
+    half_product(where_ref, grad_ref[...], weight_ref, put)
+
+
+def far(where, key_grad, weight):
+    tokens, keys = key_grad.shape
+    half = weight.shape[0]
+    vmem = pl.BlockSpec(memory_space=VMEM)
+    return pl.pallas_call(
+        far_kernel,
+        out_shape=jax.ShapeDtypeStruct((tokens, half), BF),
+        in_specs=[pl.BlockSpec(memory_space=SMEM), vmem, vmem],
+        out_specs=vmem,
+        compiler_params=pltpu.CompilerParams(vmem_limit_bytes=16 << 20),
+        cost_estimate=pl.CostEstimate(
+            flops=2 * tokens * half * keys, bytes_accessed=2 << 20, transcendentals=0
+        ),
+        name="far",
+    )(where, key_grad, weight)
+
+
+def finish_kernel(
+    my_ref, where_ref, grad_ref, near_ref, other_ref, p1, p3, begun_ref, out_ref, side, held, load_sems, sems
+):
     width = p1.shape[1]
-    y, z, core = where_ref[0], where_ref[1], where_ref[2]
-    piece = half // 8
+    half = near_ref.shape[1]
+    core = where_ref[2]
 
     def column(j):
-        return pl.multiple_of(lax.rem(my_ref[0] + 4 - j, 4) * width, width)
-
-    copies = []
-    for j, ref in ((1, p1), (3, p3)):
-        copy = pltpu.make_async_copy(ref, out_ref.at[:, pl.ds(column(j), width)], sems.at[j])
-        copy.start()
-        copies.append(copy)
-
-    def fetch(ref, row, residue):
-        turn_y = lax.rem(row + 4 - y, 4)
-        turn_z = lax.rem(residue + z, 2)
-        return ref[pl.ds(pl.multiple_of((turn_y * 2 + turn_z) * piece, piece), piece), :]
-
-    grads = grad_ref[...]
-    for source in range(2):
-        ref = near_ref if source == 0 else other_ref
-        side = core if source == 0 else 1 - core
-        for row in range(4):
-            rows = jnp.concatenate([fetch(ref, row, residue) for residue in range(2)], axis=0)
-            at = pl.multiple_of(side * half + row * 2 * piece, 2 * piece)
-            far[:, pl.ds(at, 2 * piece)] = nt(grads, rows).astype(BF)
-    copy = pltpu.make_async_copy(far, out_ref.at[:, pl.ds(column(2), width)], sems.at[2])
-    copy.start()
-    copies.append(copy)
-    for copy in copies:
-        copy.wait()
+        return lax.rem(my_ref[0] + 4 - j, 4) * width
+
+    def target(at, size):
+        return out_ref.at[:, pl.ds(pl.multiple_of(at, size), size)]
+
+    loads = [pltpu.make_async_copy(ref, held.at[i], load_sems.at[i]) for i, ref in enumerate((p1, p3))]
+    for load in loads:
+        load.start()
+    stores = [pltpu.make_async_copy(near_ref, target(column(2) + core * half, half), sems.at[0])]
+    stores[0].start()
+
+    def put(at, value):
+        side[:, at : at + value.shape[1]] = value
+
+    half_product(where_ref, grad_ref[...], other_ref, put)
+    stores.append(pltpu.make_async_copy(side, target(column(2) + (1 - core) * half, half), sems.at[1]))
+    stores[1].start()
+    for i, j in enumerate((1, 3)):
+        loads[i].wait()
+        store = pltpu.make_async_copy(held.at[i], target(column(j), width), sems.at[2 + i])
+        store.start()
+        stores.append(store)
+    for store in stores:
+        store.wait()
 
 
 def finish(my, where, key_grad, near, other, p1, p3, begun):
     tokens, width = p1.shape
     vmem = pl.BlockSpec(memory_space=VMEM)
     smem = pl.BlockSpec(memory_space=SMEM)
+    hbm = pl.BlockSpec(memory_space=pltpu.HBM)
     return pl.pallas_call(
         finish_kernel,
         out_shape=jax.ShapeDtypeStruct((tokens, 4 * width), BF),
-        in_specs=[smem, smem] + [vmem] * 5 + [pl.BlockSpec(memory_space=pltpu.HBM)],
-        out_specs=pl.BlockSpec(memory_space=pltpu.HBM),
+        in_specs=[smem, smem, vmem, vmem, vmem, hbm, hbm, hbm],
+        out_specs=hbm,
         input_output_aliases={7: 0},
-        scratch_shapes=[VMEM((tokens, width), BF), pltpu.SemaphoreType.DMA((4,))],
-        compiler_params=pltpu.CompilerParams(vmem_limit_bytes=16 << 20),
-        cost_estimate=pl.CostEstimate(flops=300_000_000, bytes_accessed=6 << 20, transcendentals=0),
+        scratch_shapes=[
+            VMEM((tokens, other.shape[0]), BF),
+            VMEM((2, tokens, width), BF),
+            pltpu.SemaphoreType.DMA((2,)),
+            pltpu.SemaphoreType.DMA((4,)),
+        ],
+        compiler_params=pltpu.CompilerParams(vmem_limit_bytes=FINISH_LIMIT << 20),
+        cost_estimate=pl.CostEstimate(flops=200_000_000, bytes_accessed=6 << 20, transcendentals=0),
         name="finish",
     )(my, where, key_grad, near, other, p1, p3, begun)
 
@@ -403,7 +445,7 @@
     table = feedback[0]
     blocks = table.shape[0]
     mean_len = blocks // owners
-    send, mask, two = prep(me, my1, kept, region_len, table, activ, key_grad, owners, width // TILE)
+    send, two = prep(me, my1, kept, region_len, table, activ, key_grad, owners)
     bundle[2] = shift(two, 2)
     plane = join([mine, twin])
     grid = [plane, None, None, None]
@@ -415,10 +457,11 @@
         back[k] = shift(part, shards - k)
     near = join(grid)
     other = turn(near, 0, 0, 1)
-    updated = grad_update(my1, activ, key_grad, [bundle[1], bundle[2], bundle[3]], [grad_one, grad_three], table, mask)
+    near_part = far(where, key_grad, near)
+    updated = grad_update(my1, activ, key_grad, [bundle[1], bundle[2], bundle[3]], [grad_one, grad_three], table, kept)
+    last = after(back[1], updated)
+    input_grad = finish(my1, where, key_grad, near_part, other, back[3], last, begun)
     owned_rows = owned(got, mean_len + mean_len // 2)
-    last = after(back[1], owned_rows, updated)
-    input_grad = finish(my1, where, key_grad, near, other, back[3], last, begun)
     return (input_grad, updated[None], owned_rows[None])
 
 

time: 92.9 us -> 93.5 us (level)
  waiting for transfers between devices: 36.5 us -> 30.9 us
  local copies, waits for them, and re-layouts: 1.74 us -> 5.3 us
  Pallas kernels: 20.7 us -> 23.1 us
    ppermute x8, waiting for transfers between devices: 21.3 us -> 15.7 us  [shift(): return lax.ppermute(x, 'shard', [(i, (i + k) % n) for i in range(n)])]
    unnamed x4 -> x14, local copies, waits for them, and re-layouts: 1.74 us -> 5.3 us
    pallas_call x0 -> x1, Pallas kernels: none -> 1.49 us  [far(): pl.pallas_call(far_kernel, out_shape=jax.ShapeDtypeStruct((tokens, half),...]
    pallas_call x1, Pallas kernels: 5.88 us -> 7.2 us  [grad_update(): pl.pallas_call(grad_kernel, out_shape=jax.ShapeDtypeStruct(table.shape, B...]
  transfers between devices with their start and end apart: 14 -> 14, of which waited for: 8 -> 8; matrix products, arithmetic and copies ran while one was open for 0% -> 0% of each run, Pallas kernels for 16% -> 19%
where the time goes in v4:
time: 93.5 us; the launch traced here: 92.7 us
  starting transfers between devices  32.3 us (35%)
  waiting for transfers between devices  30.9 us (33%)
  Pallas kernels  23.1 us (25%)
  local copies, waits for them, and re-layouts  5.3 us (6%)
    ppermute x8, waiting for transfers between devices, shift(): return lax.ppermute(x, 'shard', [(i, (i + k) % n) for i in range(n)])  15.7 us
    ppermute x5, waiting for transfers between devices, turn(): return lax.ppermute(x, 'rep', pairs)  15.2 us
    ppermute x8, starting transfers between devices, shift(): return lax.ppermute(x, 'shard', [(i, (i + k) % n) for i in range(n)])  13.7 us
    all_to_all x1, starting transfers between devices, step(): got = lax.all_to_all(send, 'rep', split_axis=0, concat_axis=0, tiled=True)  11.7 us
    pallas_call x1, Pallas kernels, grad_update(): pl.pallas_call(grad_kernel, out_shape=jax.ShapeDtypeStruct(table.shape, B...  7.2 us
    ppermute x5, starting transfers between devices, turn(): return lax.ppermute(x, 'rep', pairs)  7.01 us
    unnamed x14, local copies, waits for them, and re-layouts  5.3 us
    pallas_call x1, Pallas kernels, prep(): pl.pallas_call(prep_kernel, out_shape=(jax.ShapeDtypeStruct((owners, ROWS...  4.57 us
  transfers between devices with their start and end apart: 14, of which 8 were waited for; matrix products, arithmetic and copies ran while one was open for 0% of the time, Pallas kernels for 19%

profile of v4, /device:TPU:8, one launch (start us, length us, event | category | flops | bytes accessed | tf_op | source)
XLA Modules:
  0.0 92.7 jit_solution(1899225675032379011)
XLA Ops:
  0.7 2.3 %pack.1 = (bf16[128,2048]{1,0:T(8,128)(2,1)}, bf16[128,2048]{1,0:T(8,128)(2,1)}, bf16[128,640]{1,0:T(8,128)(2,1)}) custom-call(s32[1]{0:T(128)} %bitcast.my_ref, s32[1]{0:T(128)} %bitcast.4.index_ref, bf16[128,8192]{1,0:T(8,128)(2,1)} %a0.1, bf16[2048,640]{1,0:T(8,128)(2,1)} %weight_ref.3), custom_call_target="tpu_custom_call" | custom-call | flops 1000000 | bytes 3145728 | tf_op jit(solution)/shard_map/pack/pallas_call | solution.py:53
  3.0 3.1 %collective-permute-start = (bf16[128,640]{1,0:T(8,128)(2,1)}, bf16[128,640]{1,0:T(8,128)(2,1)S(1)}, u32[]{:S(2)}, u32[]{:S(2)}) collective-permute-start(bf16[128,640]{1,0:T(8,128)(2,1)} %get-tuple-element.12), channel_id=1, source_target_pairs={{0,2},{1,3},{2,0},{3,1},{4,6},{5,7},{6,4},{7,5},{8,10},{9,11},{10,... | collective-permute-start | bytes 491528 | tf_op jit(solution)/shard_map/ppermute | solution.py:408
  6.1 4.6 %collective-permute-done.refs_0_ = bf16[128,640]{1,0:T(8,128)(2,1)S(1)} collective-permute-done((bf16[128,640]{1,0:T(8,128)(2,1)}, bf16[128,640]{1,0:T(8,128)(2,1)S(1)}, u32[]{:S(2)}, u32[]{:S(2)}) %collective-permute-start) | collective-permute-done | bytes 163872 | tf_op jit(solution)/shard_map/ppermute | solution.py:408
  10.7 1.9 %collective-permute-start.1 = (bf16[128,640]{1,0:T(8,128)(2,1)S(1)}, bf16[128,640]{1,0:T(8,128)(2,1)S(1)}, u32[]{:S(2)}, u32[]{:S(2)}) collective-permute-start(bf16[128,640]{1,0:T(8,128)(2,1)S(1)} %collective-permute-done.refs_0_), channel_id=1, source_target_pairs={{0,8},{4,12},{8,0},{12,4},{16,24},{20,28},{24,16},{28,20},{32,40},... | collective-permute-start | bytes 491528 | tf_op jit(solution)/shard_map/ppermute | solution.py:422
  12.7 3.4 %collective-permute-done.1.refs_1_ = bf16[128,640]{1,0:T(8,128)(2,1)S(1)} collective-permute-done((bf16[128,640]{1,0:T(8,128)(2,1)S(1)}, bf16[128,640]{1,0:T(8,128)(2,1)S(1)}, u32[]{:S(2)}, u32[]{:S(2)}) %collective-permute-start.1) | collective-permute-done | bytes 163872 | tf_op jit(solution)/shard_map/ppermute | solution.py:422
  16.1 1.7 %collective-permute-start.4 = (bf16[256,640]{1,0:T(8,128)(2,1)S(1)}, bf16[256,640]{1,0:T(8,128)(2,1)S(1)}, u32[]{:S(2)}, u32[]{:S(2)}) collective-permute-start(bf16[256,640]{1,0:T(8,128)(2,1)S(1)} %join.2.refs_0_), channel_id=1, source_target_pairs={{0,64},{4,68},{8,72},{12,76},{16,80},{20,84},{24,88},{28,92},{32,9... | collective-permute-start | bytes 983048 | tf_op jit(solution)/shard_map/ppermute | solution.py:422
  17.7 2.0 %collective-permute-start.3 = (bf16[256,640]{1,0:T(8,128)(2,1)S(1)}, bf16[256,640]{1,0:T(8,128)(2,1)S(1)}, u32[]{:S(2)}, u32[]{:S(2)}) collective-permute-start(bf16[256,640]{1,0:T(8,128)(2,1)S(1)} %join.2.refs_0_), channel_id=1, source_target_pairs={{0,128},{4,132},{8,136},{12,140},{16,144},{20,148},{24,152},{28,15... | collective-permute-start | bytes 983048 | tf_op jit(solution)/shard_map/ppermute | solution.py:422
  19.8 1.3 %collective-permute-start.2 = (bf16[256,640]{1,0:T(8,128)(2,1)S(1)}, bf16[256,640]{1,0:T(8,128)(2,1)S(1)}, u32[]{:S(2)}, u32[]{:S(2)}) collective-permute-start(bf16[256,640]{1,0:T(8,128)(2,1)S(1)} %join.2.refs_0_), channel_id=1, source_target_pairs={{0,192},{4,196},{8,200},{12,204},{16,208},{20,212},{24,216},{28,22... | collective-permute-start | bytes 983048 | tf_op jit(solution)/shard_map/ppermute | solution.py:422
  21.1 5.7 %collective-permute-done.4.refs_3_ = bf16[256,640]{1,0:T(8,128)(2,1)S(1)} collective-permute-done((bf16[256,640]{1,0:T(8,128)(2,1)S(1)}, bf16[256,640]{1,0:T(8,128)(2,1)S(1)}, u32[]{:S(2)}, u32[]{:S(2)}) %collective-permute-start.4) | collective-permute-done | bytes 327712 | tf_op jit(solution)/shard_map/ppermute | solution.py:422
  26.7 3.1 %collective-permute-done.3.refs_2_ = bf16[256,640]{1,0:T(8,128)(2,1)S(1)} collective-permute-done((bf16[256,640]{1,0:T(8,128)(2,1)S(1)}, bf16[256,640]{1,0:T(8,128)(2,1)S(1)}, u32[]{:S(2)}, u32[]{:S(2)}) %collective-permute-start.3) | collective-permute-done | bytes 327712 | tf_op jit(solution)/shard_map/ppermute | solution.py:422
  29.8 3.1 %collective-permute-done.2.refs_1_ = bf16[256,640]{1,0:T(8,128)(2,1)S(1)} collective-permute-done((bf16[256,640]{1,0:T(8,128)(2,1)S(1)}, bf16[256,640]{1,0:T(8,128)(2,1)S(1)}, u32[]{:S(2)}, u32[]{:S(2)}) %collective-permute-start.2) | collective-permute-done | bytes 327712 | tf_op jit(solution)/shard_map/ppermute | solution.py:422
  32.9 0.1 join.3.weight_ref
  33.0 0.1 collective-permute-start.5
  33.1 1.6 %collective-permute-start.10 = (bf16[128,2048]{1,0:T(8,128)(2,1)}, bf16[128,2048]{1,0:T(8,128)(2,1)}, u32[]{:S(2)}, u32[]{:S(2)}) collective-permute-start(bf16[128,2048]{1,0:T(8,128)(2,1)} %get-tuple-element.15), channel_id=1, source_target_pairs={{0,1},{1,2},{2,3},{3,0},{4,5},{5,6},{6,7},{7,4},{8,9},{9,10},{10,1... | collective-permute-start | bytes 1572872 | tf_op jit(solution)/shard_map/ppermute | solution.py:408
  34.7 1.7 %collective-permute-start.7 = (bf16[128,640]{1,0:T(8,128)(2,1)}, bf16[128,640]{1,0:T(8,128)(2,1)S(1)}, u32[]{:S(2)}, u32[]{:S(2)}) collective-permute-start(bf16[128,640]{1,0:T(8,128)(2,1)} %grad_ref.5), channel_id=1, source_target_pairs={{0,3},{1,0},{2,1},{3,2},{4,7},{5,4},{6,5},{7,6},{8,11},{9,8},{10,9... | collective-permute-start | bytes 491528 | tf_op jit(solution)/shard_map/ppermute | solution.py:408
  36.4 4.6 %prep.1 = (bf16[64,24,128]{2,1,0:T(8,128)(2,1)}, bf16[128,2688]{1,0:T(8,128)(2,1)}) custom-call(s32[1]{0:T(128)} %bitcast.5.me_ref, s32[1]{0:T(128)} %bitcast.my_ref, s32[1,1,512]{2,1,0:T(1,128)} %ids_ref.3, s32[1,1,512]{2,1,0:T(1,128)} %ids_ref.3, s32[1,64]{1,0:T(1,128)} %len_ref.1, bf16[10240,128]{1,0:T(8,128)(2,1)} %bitcast.9, bf16[128,8192]{1,0:T(8,128)(2,1)} %a0.1, ...), custom_call_target="tpu_custom_call" | custom-call | flops 30000000 | bytes 5242880 | tf_op jit(solution)/shard_map/prep/pallas_call | solution.py:150
  41.0 1.9 %collective-permute-start.11 = (bf16[128,2688]{1,0:T(8,128)(2,1)}, bf16[128,2688]{1,0:T(8,128)(2,1)}, u32[]{:S(2)}, u32[]{:S(2)}) collective-permute-start(bf16[128,2688]{1,0:T(8,128)(2,1)} %get-tuple-element.16), channel_id=1, source_target_pairs={{0,2},{1,3},{2,0},{3,1},{4,6},{5,7},{6,4},{7,5},{8,10},{9,11},{10,... | collective-permute-start | bytes 2064392 | tf_op jit(solution)/shard_map/ppermute | solution.py:408
  42.9 0.6 collective-permute-start.6
  43.5 11.7 %all-to-all-start = ((bf16[64,24,128]{2,1,0:T(8,128)(2,1)}), bf16[64,24,128]{2,1,0:T(8,128)(2,1)S(1)}, u32[]{:S(2)}, u32[]{:S(2)}) async-start(bf16[64,24,128]{2,1,0:T(8,128)(2,1)} %get-tuple-element.20), calls=%async_computation | async-start | bytes 786432 | tf_op jit(solution)/shard_map/all_to_all | solution.py:454
  55.2 0.0 collective-permute-done.7.b3.g3
  55.2 2.7 %collective-permute-start.12 = (bf16[128,2048]{1,0:T(8,128)(2,1)}, bf16[128,2048]{1,0:T(8,128)(2,1)S(1)}, u32[]{:S(2)}, u32[]{:S(2)}) collective-permute-start(bf16[128,2048]{1,0:T(8,128)(2,1)} %get-tuple-element.17), channel_id=1, source_target_pairs={{0,3},{1,0},{2,1},{3,2},{4,7},{5,4},{6,5},{7,6},{8,11},{9,8},{10,9... | collective-permute-start | bytes 1572872 | tf_op jit(solution)/shard_map/ppermute | solution.py:408
  57.9 9.2 %collective-permute-done.6.b1.g1 = bf16[128,640]{1,0:T(8,128)(2,1)S(1)} collective-permute-done((bf16[128,640]{1,0:T(8,128)(2,1)}, bf16[128,640]{1,0:T(8,128)(2,1)S(1)}, u32[]{:S(2)}, u32[]{:S(2)}) %collective-permute-start.6) | collective-permute-done | bytes 163872 | tf_op jit(solution)/shard_map/ppermute | solution.py:408
  67.1 0.0 copy-start
  67.1 1.7 %copy-done = bf16[2048,640]{1,0:T(8,128)(2,1)S(1)} copy-done((bf16[2048,640]{1,0:T(8,128)(2,1)S(1)}, bf16[2048,640]{1,0:T(8,128)(2,1)}, u32[]{:S(2)}) %copy-start) | copy-done | bytes 2621464
  68.9 0.0 copy-start.3
  68.9 0.0 copy-start.5
  68.9 3.4 %dots.1 = (bf16[128,8192]{1,0:T(8,128)(2,1)}, bf16[128,2048]{1,0:T(8,128)(2,1)S(1)}, bf16[128,2048]{1,0:T(8,128)(2,1)}) custom-call(s32[1]{0:T(128)} %bitcast.my_ref, bf16[128,640]{1,0:T(8,128)(2,1)} %grad_ref.5, bf16[128,640]{1,0:T(8,128)(2,1)S(1)} %collective-permute-done.6.b1.g1, bf16[128,640]{1,0:T(8,128)(2,1)S(1)} %collective-permute-done.7.b3.g3, ...), custom_call_target="tpu_custom_call" | custom-call | flops 1006632960 | bytes 5242880 | tf_op jit(solution)/shard_map/dots/pallas_call | solution.py:296
  72.2 1.6 %collective-permute-start.9 = (bf16[128,2048]{1,0:T(8,128)(2,1)S(1)}, bf16[128,2048]{1,0:T(8,128)(2,1)S(1)}, u32[]{:S(2)}, u32[]{:S(2)}) collective-permute-start(bf16[128,2048]{1,0:T(8,128)(2,1)S(1)} %get-tuple-element.14), channel_id=1, source_target_pairs={{0,3},{1,0},{2,1},{3,2},{4,7},{5,4},{6,5},{7,6},{8,11},{9,8},{10,9... | collective-permute-start | bytes 1572872 | tf_op jit(solution)/shard_map/ppermute | solution.py:408
  73.8 0.0 collective-permute-done.10.b1
  73.8 0.4 collective-permute-start.8
  74.3 0.0 copy-done.3
  74.3 0.1 pad_add_fusion.where_ref
  74.4 1.5 %far.1.near_ref = bf16[128,1024]{1,0:T(8,128)(2,1)S(1)} custom-call(s32[3]{0:T(128)S(1)} %pad_add_fusion.where_ref, bf16[128,640]{1,0:T(8,128)(2,1)} %grad_ref.5, bf16[1024,640]{1,0:T(8,128)(2,1)S(1)} %join.3.weight_ref), custom_call_target="tpu_custom_call" | custom-call | flops 167772160 | bytes 2097152 | tf_op jit(solution)/shard_map/far/pallas_call | solution.py:337
  75.9 0.0 collective-permute-done.12.b3
  75.9 0.0 copy-start.6
  75.9 0.0 collective-permute-done.11.b2
  75.9 0.8 copy-done.6
  76.7 0.0 copy-done.5
  76.7 0.0 copy-start.4
  76.7 0.9 copy-done.4
  77.6 7.2 %grad_update.1 = bf16[10240,128]{1,0:T(8,128)(2,1)} custom-call(s32[1]{0:T(128)} %bitcast.my_ref, bf16[128,8192]{1,0:T(8,128)(2,1)} %a0.1, bf16[128,640]{1,0:T(8,128)(2,1)} %grad_ref.5, bf16[128,2048]{1,0:T(8,128)(2,1)} %collective-permute-done.10.b1, bf16[128,2688]{1,0:T(8,128)(2,1)} %collective-permute-done.11.b2, bf16[128,2048]{1,0:T(8,128)(2,1)} %copy-done.6, ...), custom_call_target="tpu_custom_call" | custom-call | flops 1342177280 | bytes 12582912 | tf_op jit(solution)/shard_map/grad_update/pallas_call | solution.py:238
  84.8 0.9 collective-permute-done.9.p3
  85.6 0.0 copy-start.1
  85.6 0.8 copy-done.1
  86.4 0.0 all-to-all-done.got_ref
  86.4 1.1 %owned.1 = f32[240,128]{1,0:T(8,128)} custom-call(bf16[64,24,128]{2,1,0:T(8,128)(2,1)S(1)} %all-to-all-done.got_ref), custom_call_target="tpu_custom_call" | custom-call | flops 4000000 | bytes 393216 | tf_op jit(solution)/shard_map/owned/pallas_call | solution.py:188
  87.5 1.0 %collective-permute-done.8.p1 = bf16[128,2048]{1,0:T(8,128)(2,1)} collective-permute-done((bf16[128,2048]{1,0:T(8,128)(2,1)}, bf16[128,2048]{1,0:T(8,128)(2,1)}, u32[]{:S(2)}, u32[]{:S(2)}) %collective-permute-start.8) | collective-permute-done | bytes 524320 | tf_op jit(solution)/shard_map/ppermute | solution.py:408
  88.5 0.0 collective-permute-done.5.other_ref
  88.5 0.0 copy-start.2
  88.5 1.0 %copy-done.2 = bf16[128,2048]{1,0:T(8,128)(2,1)S(1)} copy-done((bf16[128,2048]{1,0:T(8,128)(2,1)S(1)}, bf16[128,2048]{1,0:T(8,128)(2,1)}, u32[]{:S(2)}) %copy-start.2) | copy-done | bytes 524312
  89.5 3.0 %finish.1 = bf16[128,8192]{1,0:T(8,128)(2,1)} custom-call(s32[1]{0:T(128)} %bitcast.my_ref, s32[3]{0:T(128)S(1)} %pad_add_fusion.where_ref, bf16[128,640]{1,0:T(8,128)(2,1)} %grad_ref.5, bf16[128,1024]{1,0:T(8,128)(2,1)S(1)} %far.1.near_ref, bf16[1024,640]{1,0:T(8,128)(2,1)S(1)} %collective-permute-done.5.other_ref, ...), custom_call_target="tpu_custom_call", output_to_operand_aliasing={{}: (7, {})} | custom-call | flops 200000000 | bytes 6291456 | tf_op jit(solution)/shard_map/finish/pallas_call | solution.py:389
  (1 shorter events, 0.0 us)
Async XLA Ops:
  3.0 7.7 %collective-permute-start = (bf16[128,640]{1,0:T(8,128)(2,1)}, bf16[128,640]{1,0:T(8,128)(2,1)S(1)}, u32[]{:S(2)}, u32[]{:S(2)}) collective-permute-start(bf16[128,640]{1,0:T(8,128)(2,1)} %get-tuple-element.12), channel_id=1, source_target_pairs={{0,2},{1,3},{2,0},{3,1},{4,6},{5,7},{6,4},{7,5},{8,10},{9,11},{10,... | collective-permute-start | bytes 491528 | tf_op jit(solution)/shard_map/ppermute | solution.py:408
  10.7 5.3 %collective-permute-start.1 = (bf16[128,640]{1,0:T(8,128)(2,1)S(1)}, bf16[128,640]{1,0:T(8,128)(2,1)S(1)}, u32[]{:S(2)}, u32[]{:S(2)}) collective-permute-start(bf16[128,640]{1,0:T(8,128)(2,1)S(1)} %collective-permute-done.refs_0_), channel_id=1, source_target_pairs={{0,8},{4,12},{8,0},{12,4},{16,24},{20,28},{24,16},{28,20},{32,40},... | collective-permute-start | bytes 491528 | tf_op jit(solution)/shard_map/ppermute | solution.py:422
  16.1 10.7 %collective-permute-start.4 = (bf16[256,640]{1,0:T(8,128)(2,1)S(1)}, bf16[256,640]{1,0:T(8,128)(2,1)S(1)}, u32[]{:S(2)}, u32[]{:S(2)}) collective-permute-start(bf16[256,640]{1,0:T(8,128)(2,1)S(1)} %join.2.refs_0_), channel_id=1, source_target_pairs={{0,64},{4,68},{8,72},{12,76},{16,80},{20,84},{24,88},{28,92},{32,9... | collective-permute-start | bytes 983048 | tf_op jit(solution)/shard_map/ppermute | solution.py:422
  17.7 12.1 %collective-permute-start.3 = (bf16[256,640]{1,0:T(8,128)(2,1)S(1)}, bf16[256,640]{1,0:T(8,128)(2,1)S(1)}, u32[]{:S(2)}, u32[]{:S(2)}) collective-permute-start(bf16[256,640]{1,0:T(8,128)(2,1)S(1)} %join.2.refs_0_), channel_id=1, source_target_pairs={{0,128},{4,132},{8,136},{12,140},{16,144},{20,148},{24,152},{28,15... | collective-permute-start | bytes 983048 | tf_op jit(solution)/shard_map/ppermute | solution.py:422
  19.8 13.2 %collective-permute-start.2 = (bf16[256,640]{1,0:T(8,128)(2,1)S(1)}, bf16[256,640]{1,0:T(8,128)(2,1)S(1)}, u32[]{:S(2)}, u32[]{:S(2)}) collective-permute-start(bf16[256,640]{1,0:T(8,128)(2,1)S(1)} %join.2.refs_0_), channel_id=1, source_target_pairs={{0,192},{4,196},{8,200},{12,204},{16,208},{20,212},{24,216},{28,22... | collective-permute-start | bytes 983048 | tf_op jit(solution)/shard_map/ppermute | solution.py:422
  33.0 55.4 %collective-permute-start.5 = (bf16[1024,640]{1,0:T(8,128)(2,1)S(1)}, bf16[1024,640]{1,0:T(8,128)(2,1)S(1)}, u32[]{:S(2)}, u32[]{:S(2)}) collective-permute-start(bf16[1024,640]{1,0:T(8,128)(2,1)S(1)} %join.3.weight_ref), channel_id=1, source_target_pairs={{0,4},{4,0},{8,12},{12,8},{16,20},{20,16},{24,28},{28,24},{32,36},... | collective-permute-start | bytes 3932168 | tf_op jit(solution)/shard_map/ppermute | solution.py:422
  33.1 40.7 %collective-permute-start.10 = (bf16[128,2048]{1,0:T(8,128)(2,1)}, bf16[128,2048]{1,0:T(8,128)(2,1)}, u32[]{:S(2)}, u32[]{:S(2)}) collective-permute-start(bf16[128,2048]{1,0:T(8,128)(2,1)} %get-tuple-element.15), channel_id=1, source_target_pairs={{0,1},{1,2},{2,3},{3,0},{4,5},{5,6},{6,7},{7,4},{8,9},{9,10},{10,1... | collective-permute-start | bytes 1572872 | tf_op jit(solution)/shard_map/ppermute | solution.py:408
  34.7 20.5 %collective-permute-start.7 = (bf16[128,640]{1,0:T(8,128)(2,1)}, bf16[128,640]{1,0:T(8,128)(2,1)S(1)}, u32[]{:S(2)}, u32[]{:S(2)}) collective-permute-start(bf16[128,640]{1,0:T(8,128)(2,1)} %grad_ref.5), channel_id=1, source_target_pairs={{0,3},{1,0},{2,1},{3,2},{4,7},{5,4},{6,5},{7,6},{8,11},{9,8},{10,9... | collective-permute-start | bytes 491528 | tf_op jit(solution)/shard_map/ppermute | solution.py:408
  41.0 34.9 %collective-permute-start.11 = (bf16[128,2688]{1,0:T(8,128)(2,1)}, bf16[128,2688]{1,0:T(8,128)(2,1)}, u32[]{:S(2)}, u32[]{:S(2)}) collective-permute-start(bf16[128,2688]{1,0:T(8,128)(2,1)} %get-tuple-element.16), channel_id=1, source_target_pairs={{0,2},{1,3},{2,0},{3,1},{4,6},{5,7},{6,4},{7,5},{8,10},{9,11},{10,... | collective-permute-start | bytes 2064392 | tf_op jit(solution)/shard_map/ppermute | solution.py:408
  42.9 24.2 %collective-permute-start.6 = (bf16[128,640]{1,0:T(8,128)(2,1)}, bf16[128,640]{1,0:T(8,128)(2,1)S(1)}, u32[]{:S(2)}, u32[]{:S(2)}) collective-permute-start(bf16[128,640]{1,0:T(8,128)(2,1)} %grad_ref.5), channel_id=1, source_target_pairs={{0,1},{1,2},{2,3},{3,0},{4,5},{5,6},{6,7},{7,4},{8,9},{9,10},{10,1... | collective-permute-start | bytes 491528 | tf_op jit(solution)/shard_map/ppermute | solution.py:408
  43.5 42.9 %all-to-all-start = ((bf16[64,24,128]{2,1,0:T(8,128)(2,1)}), bf16[64,24,128]{2,1,0:T(8,128)(2,1)S(1)}, u32[]{:S(2)}, u32[]{:S(2)}) async-start(bf16[64,24,128]{2,1,0:T(8,128)(2,1)} %get-tuple-element.20), calls=%async_computation | async-start | bytes 786432 | tf_op jit(solution)/shard_map/all_to_all | solution.py:454
  55.2 20.7 %collective-permute-start.12 = (bf16[128,2048]{1,0:T(8,128)(2,1)}, bf16[128,2048]{1,0:T(8,128)(2,1)S(1)}, u32[]{:S(2)}, u32[]{:S(2)}) collective-permute-start(bf16[128,2048]{1,0:T(8,128)(2,1)} %get-tuple-element.17), channel_id=1, source_target_pairs={{0,3},{1,0},{2,1},{3,2},{4,7},{5,4},{6,5},{7,6},{8,11},{9,8},{10,9... | collective-permute-start | bytes 1572872 | tf_op jit(solution)/shard_map/ppermute | solution.py:408
  67.1 1.7 %copy-start = (bf16[2048,640]{1,0:T(8,128)(2,1)S(1)}, bf16[2048,640]{1,0:T(8,128)(2,1)}, u32[]{:S(2)}) copy-start(bf16[2048,640]{1,0:T(8,128)(2,1)} %weight_ref.3) | copy-start | bytes 7864324
  68.9 5.4 %copy-start.3 = (bf16[128,640]{1,0:T(8,128)(2,1)}, bf16[128,640]{1,0:T(8,128)(2,1)S(1)}, u32[]{:S(2)}) copy-start(bf16[128,640]{1,0:T(8,128)(2,1)S(1)} %collective-permute-done.6.b1.g1) | copy-start | bytes 491524
  68.9 7.8 %copy-start.5 = (s32[1,1,512]{2,1,0:T(1,128)S(1)}, s32[1,1,512]{2,1,0:T(1,128)}, u32[]{:S(2)}) copy-start(s32[1,1,512]{2,1,0:T(1,128)} %ids_ref.3) | copy-start | bytes 6148
  72.2 13.4 %collective-permute-start.9 = (bf16[128,2048]{1,0:T(8,128)(2,1)S(1)}, bf16[128,2048]{1,0:T(8,128)(2,1)S(1)}, u32[]{:S(2)}, u32[]{:S(2)}) collective-permute-start(bf16[128,2048]{1,0:T(8,128)(2,1)S(1)} %get-tuple-element.14), channel_id=1, source_target_pairs={{0,3},{1,0},{2,1},{3,2},{4,7},{5,4},{6,5},{7,6},{8,11},{9,8},{10,9... | collective-permute-start | bytes 1572872 | tf_op jit(solution)/shard_map/ppermute | solution.py:408
  73.8 14.6 %collective-permute-start.8 = (bf16[128,2048]{1,0:T(8,128)(2,1)}, bf16[128,2048]{1,0:T(8,128)(2,1)}, u32[]{:S(2)}, u32[]{:S(2)}) collective-permute-start(bf16[128,2048]{1,0:T(8,128)(2,1)} %get-tuple-element.13), channel_id=1, source_target_pairs={{0,1},{1,2},{2,3},{3,0},{4,5},{5,6},{6,7},{7,4},{8,9},{9,10},{10,1... | collective-permute-start | bytes 1572872 | tf_op jit(solution)/shard_map/ppermute | solution.py:408
  75.9 0.8 copy-start.6
  76.7 0.9 copy-start.4
  85.6 0.8 copy-start.1
  88.5 1.0 %copy-start.2 = (bf16[128,2048]{1,0:T(8,128)(2,1)S(1)}, bf16[128,2048]{1,0:T(8,128)(2,1)}, u32[]{:S(2)}) copy-start(bf16[128,2048]{1,0:T(8,128)(2,1)} %copy-done.1) | copy-start | bytes 1572868
